TPU v7x, 64 devices: a 2x2x8 block of a 4x4x8 slice. The times are simulated.
64 devices in a mesh: rep: 8 (over x, y, core), dp: 8 (over z).
Axes of the slice: x: 2, y: 2, z: 8, core: 2. Of those that a mesh axis runs over, the one named last changes fastest.
The devices are a block of a 4x4x8 slice.
Arguments:
- x: bfloat16 [64, 4096, 512], P(('rep', 'dp')), parts along dimension 0
- dy: bfloat16 [64, 4096, 512], P(('rep', 'dp')), parts along dimension 0
- w_gate: bfloat16 [2, 512, 1664], P(None, 'dp')
- w_up: bfloat16 [2, 512, 1664], P(None, 'dp')
- w_down: bfloat16 [2, 1664, 512], P(None, 'dp')
- m_w_gate: float32 [2, 512, 1664], P(None, 'dp')
- m_w_up: float32 [2, 512, 1664], P(None, 'dp')
- m_w_down: float32 [2, 1664, 512], P(None, 'dp')
- v_w_gate: float32 [2, 512, 1664], P(None, 'dp')
- v_w_up: float32 [2, 512, 1664], P(None, 'dp')
- v_w_down: float32 [2, 1664, 512], P(None, 'dp')
Outputs:
- output 1: bfloat16 [16, 512, 1664], P('rep', 'dp'), parts along dimension 0
- output 2: bfloat16 [16, 512, 1664], P('rep', 'dp'), parts along dimension 0
- output 3: bfloat16 [16, 1664, 512], P('rep', 'dp'), parts along dimension 0
- output 4: float32 [16, 512, 1664], P('rep', 'dp'), parts along dimension 0
- output 5: float32 [16, 512, 1664], P('rep', 'dp'), parts along dimension 0
- output 6: float32 [16, 1664, 512], P('rep', 'dp'), parts along dimension 0
- output 7: float32 [16, 512, 1664], P('rep', 'dp'), parts along dimension 0
- output 8: float32 [16, 512, 1664], P('rep', 'dp'), parts along dimension 0
- output 9: float32 [16, 1664, 512], P('rep', 'dp'), parts along dimension 0
There are 8 independent parts. A program takes and returns all parts, laid end to end along the dimension named above; an argument that names none is the same for every part.
All inputs are finite; a program needn't handle non-finite values.
Results may differ from a plain program's by a relative error of at most 0.0202.
Values are sent between devices in bfloat16 or wider.
A program may use at most 768 MiB of HBM per device.

v0:
```python
import jax
import jax.numpy as jnp
from jax import lax
from jax.sharding import PartitionSpec as P

NAMES = ("w_gate", "w_up", "w_down")


def matmul(a, w):
    return jnp.dot(a, w, preferred_element_type=jnp.float32).astype(jnp.bfloat16)


def normed(h):
    wide = h.astype(jnp.float32)
    scale = lax.rsqrt(jnp.mean(wide**2, -1, keepdims=True) + 1e-6)
    return (wide * scale).astype(jnp.bfloat16)


def layer(h, w):
    a = normed(h)
    gate = jnp.dot(a, w["w_gate"], preferred_element_type=jnp.float32)
    up = jnp.dot(a, w["w_up"], preferred_element_type=jnp.float32)
    return h + matmul((jax.nn.silu(gate) * up).astype(jnp.bfloat16), w["w_down"])


def adamw(w, m, v, g):
    m = 0.9 * m + 0.1 * g
    v = 0.95 * v + 0.05 * g * g
    step = m * lax.rsqrt(v + 1e-8) + 0.1 * w
    return (w - 0.02 * step).astype(jnp.bfloat16), m, v


def solution(mesh):
    def fetched(weights, number):
        return {name: lax.all_gather(w[number], "dp", axis=0, tiled=True) for name, w in zip(NAMES, weights, strict=True)}

    def step(x, dy, *arrays):
        weights, m, v = (arrays[i : i + 3] for i in (0, 3, 6))
        layers = weights[0].shape[0]
        h, kept = x[0], []
        for number in range(layers):
            kept.append(h)
            h = layer(h, fetched(weights, number))
        by_h, mine = dy[0], [None] * layers
        for number in reversed(range(layers)):
            _, back = jax.vjp(lambda w, h: layer(h, w), fetched(weights, number), kept[number])
            by_w, by_h = back(by_h)
            mine[number] = [lax.psum_scatter(by_w[name], "dp", scatter_dimension=0, tiled=True) for name in NAMES]
        gradients = [jnp.stack([mine[number][i] for number in range(layers)]).astype(jnp.float32) for i in range(3)]
        new = [adamw(w.astype(jnp.float32), m, v, g) for w, m, v, g in zip(weights, m, v, gradients, strict=True)]
        return tuple(one[which] for which in range(3) for one in new)

    states, cut = P(("rep", "dp"), None, None), P(None, "dp", None)
    return jax.shard_map(
        step,
        mesh=mesh,
        in_specs=(states, states) + (cut,) * 9,
        out_specs=(P("rep", "dp", None),) * 9,
        check_vma=False,
    )
```

profile of v0, /device:TPU:22, one launch (start us, length us, event | category | flops | bytes accessed | tf_op | source)
XLA Modules:
  0.0 563.3 jit_solution(1574933615888857562)
XLA Ops:
  7.3 1.8 fusion.87
  15.0 6.5 %copy.20 = bf16[1,4096,512]{1,2,0:T(8,128)(2,1)} copy(bf16[1,4096,512]{2,1,0:T(8,128)(2,1)} %param.11) | data formatting | bytes 8388608 | tf_op args[0]
  21.5 3.1 fusion.15
  24.6 6.5 %copy.21 = bf16[1,4096,512]{1,2,0:T(8,128)(2,1)} copy(bf16[1,4096,512]{2,1,0:T(8,128)(2,1)} %param.12) | data formatting | bytes 8388608 | tf_op args[1]
  31.1 19.3 %all-gather.13.cloned.1.call-done = bf16[1,512,1664]{2,1,0:T(8,128)(2,1)} async-done(((bf16[1,64,1664]{2,1,0:T(8,128)(2,1)}), bf16[1,512,1664]{2,1,0:T(8,128)(2,1)}) %all-gather.13.cloned.1.call-update) | async-done | bytes 1703952 | tf_op jit(solution)/shard_map/all_gather | solution.py:35
  50.4 15.1 %fusion.47 = f32[4096,1664]{1,0:T(8,128)} fusion(bf16[1,4096,512]{1,2,0:T(8,128)(2,1)} %copy.20, f32[4096]{0:T(1024)S(1)} %add_rsqrt_fusion, bf16[1,512,1664]{2,1,0:T(8,128)(2,1)} %all-gather.13.cloned.1.call-done), kind=kOutput, calls=%fused_computation.57 | convolution fusion | flops 6985613312 | bytes 33177600 | tf_op jit(solution)/shard_map/dot_general | solution.py:21
  65.6 22.2 %all-gather.15.cloned.1.call-done = bf16[1,512,1664]{2,1,0:T(8,128)(2,1)} async-done(((bf16[1,64,1664]{2,1,0:T(8,128)(2,1)}), bf16[1,512,1664]{2,1,0:T(8,128)(2,1)}) %all-gather.15.cloned.1.call-update) | async-done | bytes 1703952 | tf_op jit(solution)/shard_map/all_gather | solution.py:35
  87.7 27.6 %multiply_convert_fusion.1 = (bf16[4096,1664]{1,0:T(8,128)(2,1)}, f32[4096,1664]{1,0:T(8,128)}) fusion(f32[4096,1664]{1,0:T(8,128)} %fusion.47, bf16[1,512,1664]{2,1,0:T(8,128)(2,1)} %all-gather.15.cloned.1.call-done, bf16[1,4096,512]{1,2,0:T(8,128)(2,1)} %copy.20, f32[4096]{0:T(1024)S(1)} %add_rsqrt_fusion), kind=kOutput, calls=%fused_computation.17 | convolution fusion | flops 7026507776 | bytes 74072064 | tf_op jit(solution)/shard_map/dot_general | solution.py:22
  115.4 9.7 %all-gather.17.cloned.1.call-done = bf16[1,1664,512]{2,1,0:T(8,128)(2,1)} async-done(((bf16[1,208,512]{2,1,0:T(8,128)(2,1)}), bf16[1,1664,512]{2,1,0:T(8,128)(2,1)}) %all-gather.17.cloned.1.call-update) | async-done | bytes 1703952 | tf_op jit(solution)/shard_map/all_gather | solution.py:35
  125.0 14.2 %fusion.19 = (f32[4096]{0:T(1024)S(1)}, bf16[4096,512]{0,1:T(8,128)(2,1)}) fusion(bf16[4096,1664]{1,0:T(8,128)(2,1)} %get-tuple-element.24, bf16[1,1664,512]{2,1,0:T(8,128)(2,1)} %all-gather.17.cloned.1.call-done, bf16[1,4096,512]{1,2,0:T(8,128)(2,1)} %copy.20), kind=kOutput, calls=%fused_computation.37 | convolution fusion | flops 6989803520 | bytes 23740416 | tf_op jit(solution)/shard_map/dot_general | solution.py:10
  139.9 22.3 %all-gather.21.cloned.1.call-done = bf16[1,1664,512]{2,1,0:T(8,128)(2,1)} async-done(((bf16[1,208,512]{2,1,0:T(8,128)(2,1)}), bf16[1,1664,512]{2,1,0:T(8,128)(2,1)}) %all-gather.21.cloned.1.call-update) | async-done | bytes 1703952 | tf_op jit(solution)/shard_map/all_gather | solution.py:35
  162.2 12.9 %convolution_convert_fusion.1 = bf16[4096,1664]{1,0:T(8,128)(2,1)} fusion(bf16[1,4096,512]{2,1,0:T(8,128)(2,1)} %param.12, bf16[1,1664,512]{2,1,0:T(8,128)(2,1)} %all-gather.21.cloned.1.call-done), kind=kOutput, calls=%fused_computation.23 | convolution fusion | flops 6986137600 | bytes 19529728 | tf_op jit(solution)/shard_map/transpose(jvp())/dot_general | solution.py:10
  175.1 24.3 %all-gather.23.cloned.1.call-done = bf16[1,512,1664]{2,1,0:T(8,128)(2,1)} async-done(((bf16[1,64,1664]{2,1,0:T(8,128)(2,1)}), bf16[1,512,1664]{2,1,0:T(8,128)(2,1)}) %all-gather.23.cloned.1.call-update) | async-done | bytes 1703952 | tf_op jit(solution)/shard_map/all_gather | solution.py:35
  199.3 15.0 %fusion.39 = f32[4096,1664]{1,0:T(8,128)} fusion(bf16[4096,512]{0,1:T(8,128)(2,1)} %get-tuple-element.27, f32[4096]{0:T(1024)S(1)} %fusion.73, bf16[1,512,1664]{2,1,0:T(8,128)(2,1)} %all-gather.23.cloned.1.call-done), kind=kOutput, calls=%fused_computation.54 | convolution fusion | flops 6985613312 | bytes 33177600 | tf_op jit(solution)/shard_map/jvp()/dot_general | solution.py:22
  214.4 22.1 %all-gather.19.cloned.1.call-done = bf16[1,512,1664]{2,1,0:T(8,128)(2,1)} async-done(((bf16[1,64,1664]{2,1,0:T(8,128)(2,1)}), bf16[1,512,1664]{2,1,0:T(8,128)(2,1)}) %all-gather.19.cloned.1.call-update) | async-done | bytes 1703952 | tf_op jit(solution)/shard_map/all_gather | solution.py:35
  236.5 36.8 %fusion.2 = (bf16[4096,1664]{1,0:T(8,128)(2,1)}, f32[4096,1664]{1,0:T(8,128)}) fusion(f32[4096,1664]{1,0:T(8,128)} %fusion.39, bf16[4096,1664]{1,0:T(8,128)(2,1)} %convolution_convert_fusion.1, bf16[1,512,1664]{2,1,0:T(8,128)(2,1)} %all-gather.19.cloned.1.call-done, bf16[4096,512]{0,1:T(8,128)(2,1)} %get-tuple-element.27, f32[4096]{0:T(1024)S(1)} %fusion.73), kind=kOutput, calls=%fused_computation.8 | convolution fusion | flops 7067402240 | bytes 87703552 | tf_op jit(solution)/shard_map/jvp()/dot_general | solution.py:21
  273.3 14.5 %convolution_convert_fusion.4 = bf16[512,1664]{1,0:T(8,128)(2,1)} fusion(bf16[4096,1664]{1,0:T(8,128)(2,1)} %get-tuple-element.28, bf16[4096,512]{0,1:T(8,128)(2,1)} %get-tuple-element.27, f32[4096]{0:T(1024)S(1)} %fusion.73), kind=kOutput, calls=%fused_computation.49 | convolution fusion | flops 6985613312 | bytes 19546112 | tf_op jit(solution)/shard_map/transpose(jvp())/dot_general | solution.py:21
  287.9 19.3 %fusion.22 = bf16[4096,512]{0,1:T(8,128)(2,1)} fusion(bf16[4096,1664]{1,0:T(8,128)(2,1)} %convolution_convert_fusion.1, bf16[1,512,1664]{2,1,0:T(8,128)(2,1)S(1)} %copy-done.14, f32[4096,1664]{1,0:T(8,128)} %get-tuple-element.29), kind=kOutput, calls=%fused_computation.40 | convolution fusion | flops 7022313472 | bytes 46792704 | tf_op jit(solution)/shard_map/transpose(jvp())/dot_general | solution.py:22
  307.2 13.7 %fusion.21 = (f32[4096]{0:T(1024)S(1)}, bf16[4096,512]{0,1:T(8,128)(2,1)S(1)}) fusion(bf16[4096,512]{0,1:T(8,128)(2,1)} %get-tuple-element.27, bf16[4096,512]{0,1:T(8,128)(2,1)} %fusion.22, bf16[4096,1664]{1,0:T(8,128)(2,1)} %get-tuple-element.28, bf16[1,512,1664]{2,1,0:T(8,128)(2,1)} %all-gather.19.cloned.1.call-done), kind=kOutput, calls=%fused_computation.39 | convolution fusion | flops 6989803520 | bytes 27934720 | tf_op jit(solution)/shard_map/transpose(jvp())/dot_general | solution.py:21
  321.0 3.1 fusion.26
  324.2 11.2 %convolution_convert_fusion = bf16[4096,1664]{1,0:T(8,128)(2,1)} fusion(bf16[4096,512]{0,1:T(8,128)(2,1)S(1)} %fusion.26, bf16[1,1664,512]{2,1,0:T(8,128)(2,1)S(1)} %copy-done.13), kind=kOutput, calls=%fused_computation.22 | convolution fusion | flops 6986137600 | bytes 19529728 | tf_op jit(solution)/shard_map/transpose(jvp())/dot_general | solution.py:10
  335.4 25.7 %fusion.34 = bf16[512,1664]{1,0:T(8,128)(2,1)} fusion(f32[4096,1664]{1,0:T(8,128)} %fusion.47, f32[4096,1664]{1,0:T(8,128)} %get-tuple-element.25, bf16[4096,1664]{1,0:T(8,128)(2,1)} %convolution_convert_fusion, bf16[1,4096,512]{1,2,0:T(8,128)(2,1)S(1)} %copy-done, f32[4096]{0:T(1024)S(1)} %copy-done.12), kind=kOutput, calls=%fused_computation.53 | convolution fusion | flops 7061438464 | bytes 74072064 | tf_op jit(solution)/shard_map/transpose(jvp())/dot_general | solution.py:21
  361.3 20.2 %fusion.33 = bf16[512,1664]{1,0:T(8,128)(2,1)} fusion(bf16[4096,1664]{1,0:T(8,128)(2,1)} %convolution_convert_fusion.1, bf16[4096,512]{0,1:T(8,128)(2,1)} %get-tuple-element.27, f32[4096]{0:T(1024)S(1)} %fusion.73, f32[4096,1664]{1,0:T(8,128)} %get-tuple-element.29), kind=kOutput, calls=%fused_computation.51 | convolution fusion | flops 7027359744 | bytes 46809088 | tf_op jit(solution)/shard_map/transpose(jvp())/dot_general | solution.py:22
  381.6 19.8 %fusion.29 = bf16[512,1664]{1,0:T(8,128)(2,1)} fusion(bf16[4096,1664]{1,0:T(8,128)(2,1)} %convolution_convert_fusion, f32[4096,1664]{1,0:T(8,128)} %fusion.47, bf16[1,4096,512]{1,2,0:T(8,128)(2,1)} %copy.20, f32[4096]{0:T(1024)S(1)} %copy-done.12), kind=kOutput, calls=%fused_computation.48 | convolution fusion | flops 7027359744 | bytes 46809088 | tf_op jit(solution)/shard_map/transpose(jvp())/dot_general | solution.py:22
  401.5 23.0 %fusion.30 = bf16[1664,512]{1,0:T(8,128)(2,1)} fusion(bf16[1,4096,512]{2,1,0:T(8,128)(2,1)} %param.12, f32[4096,1664]{1,0:T(8,128)} %fusion.39, f32[4096,1664]{1,0:T(8,128)} %get-tuple-element.29), kind=kOutput, calls=%fused_computation.50 | convolution fusion | flops 7021068288 | bytes 60424192 | tf_op jit(solution)/shard_map/transpose(jvp())/dot_general | solution.py:10
  424.7 14.1 %convolution_convert_fusion.5 = bf16[1664,512]{1,0:T(8,128)(2,1)} fusion(bf16[4096,1664]{1,0:T(8,128)(2,1)} %get-tuple-element.24, bf16[4096,512]{0,1:T(8,128)(2,1)} %copy-done.3), kind=kOutput, calls=%fused_computation.52 | convolution fusion | flops 6980173824 | bytes 19529728 | tf_op jit(solution)/shard_map/transpose(jvp())/dot_general | solution.py:10
  439.0 2.6 fusion.60
  441.5 33.7 %reduce-scatter.11.cloned.1.call-done = bf16[64,1664]{1,0:T(8,128)(2,1)} async-done(((bf16[512,1664]{1,0:T(8,128)(2,1)}), bf16[64,1664]{1,0:T(8,128)(2,1)}) %reduce-scatter.11.cloned.1.call-update) | async-done | bytes 213008 | tf_op jit(solution)/shard_map/reduce_scatter | solution.py:48
  475.3 3.2 fusion.64
  478.4 35.6 %reduce-scatter.17.cloned.1.call-done = bf16[208,512]{1,0:T(8,128)(2,1)} async-done(((bf16[1664,512]{1,0:T(8,128)(2,1)}), bf16[208,512]{1,0:T(8,128)(2,1)}) %reduce-scatter.17.cloned.1.call-update) | async-done | bytes 213008 | tf_op jit(solution)/shard_map/reduce_scatter | solution.py:48
  514.0 38.7 %reduce-scatter.15.cloned.1.call-done = bf16[208,512]{1,0:T(8,128)(2,1)} async-done(((bf16[1664,512]{1,0:T(8,128)(2,1)}), bf16[208,512]{1,0:T(8,128)(2,1)}) %reduce-scatter.15.cloned.1.call-update) | async-done | bytes 213008 | tf_op jit(solution)/shard_map/reduce_scatter | solution.py:48
  552.7 3.2 fusion.68
  (62 shorter events, 7.3 us)
Async XLA Ops:
  7.2 43.2 %all-gather.13.cloned.1.call-start = ((), (), s32[]{:S(2)}) async-start(), calls=%async_computation.12 | async-start | bytes 1916928 | tf_op jit(solution)/shard_map/all_gather | solution.py:35
  9.1 78.6 %all-gather.15.cloned.1.call-start = ((), (), s32[]{:S(2)}) async-start(), calls=%async_computation.13 | async-start | bytes 1916928 | tf_op jit(solution)/shard_map/all_gather | solution.py:35
  11.1 113.9 %all-gather.17.cloned.1.call-start = ((), (), s32[]{:S(2)}) async-start(), calls=%async_computation.14 | async-start | bytes 1916928 | tf_op jit(solution)/shard_map/all_gather | solution.py:35
  13.1 149.1 %all-gather.21.cloned.1.call-start = ((), (), s32[]{:S(2)}) async-start(), calls=%async_computation.16 | async-start | bytes 1916928 | tf_op jit(solution)/shard_map/all_gather | solution.py:35
  13.7 185.6 %all-gather.23.cloned.1.call-start = ((), (), s32[]{:S(2)}) async-start(), calls=%async_computation.17 | async-start | bytes 1916928 | tf_op jit(solution)/shard_map/all_gather | solution.py:35
  14.3 222.1 %all-gather.19.cloned.1.call-start = ((), (), s32[]{:S(2)}) async-start(), calls=%async_computation.15 | async-start | bytes 1916928 | tf_op jit(solution)/shard_map/all_gather | solution.py:35
  15.0 423.9 %reduce-scatter.9.cloned.1.call-start = ((), (), s32[]{:S(2)}) async-start(), calls=%async_computation.7 | async-start | bytes 1916928 | tf_op jit(solution)/shard_map/reduce_scatter | solution.py:48
  24.6 63.1 %copy-start.11 = (f32[4096]{0:T(1024)}, f32[4096]{0:T(1024)S(1)}, u32[]{:S(2)}) copy-start(f32[4096]{0:T(1024)S(1)} %add_rsqrt_fusion) | copy-start | bytes 49156
  139.2 0.6 copy-start.9
  273.3 14.6 %copy-start.14 = (bf16[1,512,1664]{2,1,0:T(8,128)(2,1)S(1)}, bf16[1,512,1664]{2,1,0:T(8,128)(2,1)}, u32[]{:S(2)}) copy-start(bf16[1,512,1664]{2,1,0:T(8,128)(2,1)} %all-gather.23.cloned.1.call-done) | copy-start | bytes 5111812
  287.8 151.1 %reduce-scatter.7.cloned.1.call-start = ((), (), s32[]{:S(2)}) async-start(), calls=%async_computation.6 | async-start | bytes 1916928 | tf_op jit(solution)/shard_map/reduce_scatter | solution.py:48
  307.2 13.8 %copy-start.10 = (f32[4096]{0:T(1024)S(1)}, f32[4096]{0:T(1024)}, u32[]{:S(2)}) copy-start(f32[4096]{0:T(1024)} %copy-done.9) | copy-start | bytes 49156
  307.2 13.8 %copy-start.1 = (bf16[1,4096,512]{1,2,0:T(8,128)(2,1)S(1)}, bf16[1,4096,512]{1,2,0:T(8,128)(2,1)}, u32[]{:S(2)}) copy-start(bf16[1,4096,512]{1,2,0:T(8,128)(2,1)} %copy.21) | copy-start | bytes 12582916
  307.2 13.8 %copy-start.2 = (bf16[4096,512]{0,1:T(8,128)(2,1)S(1)}, bf16[4096,512]{0,1:T(8,128)(2,1)}, u32[]{:S(2)}) copy-start(bf16[4096,512]{0,1:T(8,128)(2,1)} %get-tuple-element.27) | copy-start | bytes 12582916
  321.0 3.2 copy-start.13
  324.2 11.2 %copy-start.3 = (bf16[4096,512]{0,1:T(8,128)(2,1)}, bf16[4096,512]{0,1:T(8,128)(2,1)S(1)}, u32[]{:S(2)}) copy-start(bf16[4096,512]{0,1:T(8,128)(2,1)S(1)} %fusion.26) | copy-start | bytes 12582916
  324.2 11.2 %copy-start = (bf16[1,4096,512]{1,2,0:T(8,128)(2,1)S(1)}, bf16[1,4096,512]{1,2,0:T(8,128)(2,1)}, u32[]{:S(2)}) copy-start(bf16[1,4096,512]{1,2,0:T(8,128)(2,1)} %copy.20) | copy-start | bytes 12582916
  324.2 11.2 %copy-start.12 = (f32[4096]{0:T(1024)S(1)}, f32[4096]{0:T(1024)}, u32[]{:S(2)}) copy-start(f32[4096]{0:T(1024)} %copy-done.11) | copy-start | bytes 49156
  361.2 80.3 %reduce-scatter.13.cloned.1.call-start = ((), (), s32[]{:S(2)}) async-start(), calls=%async_computation.9 | async-start | bytes 1916928 | tf_op jit(solution)/shard_map/reduce_scatter | solution.py:48
  381.5 93.7 %reduce-scatter.11.cloned.1.call-start = ((), (), s32[]{:S(2)}) async-start(), calls=%async_computation.8 | async-start | bytes 1916928 | tf_op jit(solution)/shard_map/reduce_scatter | solution.py:48
  401.5 112.6 %reduce-scatter.17.cloned.1.call-start = ((), (), s32[]{:S(2)}) async-start(), calls=%async_computation.11 | async-start | bytes 1916928 | tf_op jit(solution)/shard_map/reduce_scatter | solution.py:48
  424.6 14.4 %copy-start.4 = (bf16[2,64,1664]{2,1,0:T(8,128)(2,1)S(1)}, bf16[2,64,1664]{2,1,0:T(8,128)(2,1)}, u32[]{:S(2)}) copy-start(bf16[2,64,1664]{2,1,0:T(8,128)(2,1)} %param.13) | copy-start | bytes 1277956
  424.6 14.4 %copy-start.7 = (f32[2,64,1664]{2,1,0:T(8,128)S(1)}, f32[2,64,1664]{2,1,0:T(8,128)}, u32[]{:S(2)}) copy-start(f32[2,64,1664]{2,1,0:T(8,128)} %param.19) | copy-start | bytes 2555908
  424.6 14.4 %copy-start.8 = (f32[2,64,1664]{2,1,0:T(8,128)S(1)}, f32[2,64,1664]{2,1,0:T(8,128)}, u32[]{:S(2)}) copy-start(f32[2,64,1664]{2,1,0:T(8,128)} %param.16) | copy-start | bytes 2555908
  424.6 50.7 %copy-start.5 = (bf16[2,64,1664]{2,1,0:T(8,128)(2,1)S(1)}, bf16[2,64,1664]{2,1,0:T(8,128)(2,1)}, u32[]{:S(2)}) copy-start(bf16[2,64,1664]{2,1,0:T(8,128)(2,1)} %param.14) | copy-start | bytes 1277956
  424.6 128.1 %reduce-scatter.15.cloned.1.call-start = ((), (), s32[]{:S(2)}) async-start(), calls=%async_computation.10 | async-start | bytes 1916928 | tf_op jit(solution)/shard_map/reduce_scatter | solution.py:48
  438.8 113.9 %copy-start.6 = (bf16[2,208,512]{2,1,0:T(8,128)(2,1)S(1)}, bf16[2,208,512]{2,1,0:T(8,128)(2,1)}, u32[]{:S(2)}) copy-start(bf16[2,208,512]{2,1,0:T(8,128)(2,1)} %param.15) | copy-start | bytes 1277956
Sparse Core Ops, SparseCore 0:
  10.2 40.1 all-gather.12
  52.6 35.0 all-gather.14
  89.9 35.0 all-gather.16
  127.0 35.0 all-gather.20
  164.2 35.0 all-gather.22
  201.3 35.0 all-gather.18
  288.0 36.3 reduce-scatter.8
  361.3 36.3 reduce-scatter.6
  400.1 36.4 reduce-scatter.12
  438.8 36.4 reduce-scatter.10
  477.6 36.3 reduce-scatter.16
  516.2 36.4 reduce-scatter.14
where the time goes:
time: 571 us; the launch traced here: 563 us
  matrix products  283 us (50%)
  waiting for transfers between devices  230 us (40%)
  local copies, waits for them, and re-layouts  19.1 us (3%)
  other arithmetic  15.2 us (3%)
  between operations  14.9 us (3%)
    all_gather x6, waiting for transfers between devices, fetched(): lax.all_gather(w[number], 'dp', axis=0, tiled=True)  120 us
    reduce_scatter x6, waiting for transfers between devices, step(): lax.psum_scatter(by_w[name], 'dp', scatter_dimension=0, tiled=True)  108 us
    dot_general x5, matrix products, layer(): gate = jnp.dot(a, w['w_gate'], preferred_element_type=jnp.float32)  106 us
    dot_general x5, matrix products, layer(): up = jnp.dot(a, w['w_up'], preferred_element_type=jnp.float32)  102 us
    dot_general x5, matrix products, matmul(): jnp.dot(a, w, preferred_element_type=jnp.float32).astype(jnp.bfloat16)  75.4 us
    unnamed x32, local copies, waits for them, and re-layouts  13.6 us
  transfers between devices with their start and end apart: 12, of which 9 were waited for; matrix products, arithmetic and copies ran while one was open for 46% of the time, Pallas kernels for 0%

commit v1 on v0

v1 whole, which is shorter than its diff:
```python
import functools

import jax
import jax.numpy as jnp
from jax import lax
from jax.experimental import pallas as pl
from jax.experimental.pallas import tpu as pltpu
from jax.sharding import PartitionSpec as P

BF16, F32 = jnp.bfloat16, jnp.float32
MESH = pl.DeviceIdType.MESH
TILE = 512
CHUNK = 256
GROUP = 2
VMEM_LIMIT = 63 * 1024 * 1024


def dot(a, b):
    return jnp.dot(a, b, preferred_element_type=F32)


def scale_of(wide):
    return lax.rsqrt(jnp.mean(wide * wide, -1, keepdims=True) + 1e-6)


def sigmoid(g):
    return 0.5 * jnp.tanh(0.5 * g) + 0.5


def adamw(w, m, v, g):
    m = 0.9 * m + 0.1 * g
    v = 0.95 * v + 0.05 * g * g
    step = m * lax.rsqrt(v + 1e-8) + 0.1 * w
    return (w - 0.02 * step).astype(BF16), m, v


def tile_rows(t):
    return pl.ds(pl.multiple_of(t * TILE, TILE), TILE)


def greet(others):
    barrier = pltpu.get_barrier_semaphore()
    for other in others:
        pl.semaphore_signal(barrier, inc=1, device_id=other, device_id_type=MESH)
    pl.semaphore_wait(barrier, len(others))


def forward_kernel(
    n, x_ref, gate_ref, up_ref, down_ref, h_ref, gu0_out, d0_out, gu1_out, d1_out,
    gu, dn, hid, own_sem, out_sem, send_sem, recv_sem, psend_sem, precv_sem,
):
    me = lax.axis_index("dp")
    rep = lax.axis_index("rep")
    core = lax.rem(rep, 2)
    right, left = {"dp": lax.rem(me + 1, n)}, {"dp": lax.rem(me + n - 1, n)}
    partner = {"rep": rep + 1 - 2 * core}
    layers, rows, ff = gate_ref.shape
    drows, d = down_ref.shape[1:]
    half, quarter = d // 2, d // 4

    def own(l):
        mine = pl.ds(pl.multiple_of(me * rows, rows), rows)
        down = pl.ds(pl.multiple_of(me * drows, 16), drows)
        return (
            pltpu.make_async_copy(gate_ref.at[l], gu.at[l, 0, mine], own_sem.at[l, 0]),
            pltpu.make_async_copy(up_ref.at[l], gu.at[l, 1, mine], own_sem.at[l, 1]),
            pltpu.make_async_copy(down_ref.at[l], dn.at[l, down], own_sem.at[l, 2]),
        )

    for l in range(layers):
        for copy in own(l):
            copy.start()
    greet((right, left, partner))

    def piece(l, c, side, part, k):
        if part == 0:
            start = pl.multiple_of(k * rows + side * (rows // 2), rows // 2)
            return gu.at[l, c, pl.ds(start, rows // 2)]
        start = pl.multiple_of(k * drows, 16)
        return dn.at[l, pl.ds(start, drows), pl.ds(pl.multiple_of(c * half + side * quarter, quarter), quarter)]

    def ring(l, side, part, s, k):
        ref = piece(l, core, side, part, k)
        return pltpu.make_async_remote_copy(
            ref, ref, send_sem.at[l, side, part, s], recv_sem.at[l, side, part, s], (right, left)[side], MESH
        )

    def across(l, c, side, part, s, k):
        ref = piece(l, c, side, part, k)
        return pltpu.make_async_remote_copy(
            ref, ref, psend_sem.at[l, side, part, s], precv_sem.at[l, side, part, s], partner, MESH
        )

    def holder(side, s):
        return lax.rem(me + n - s, n) if side == 0 else lax.rem(me + s, n)

    def gather_step(l, s):
        for part in range(2):
            for side in range(2):
                k = holder(side, s)

                @pl.when(s > 0)
                def _():
                    ring(l, side, part, s - 1, k).wait_recv()

                @pl.when(s < n - 1)
                def _():
                    ring(l, side, part, s, k).start()

                @pl.when(s > 0)
                def _():
                    across(l, core, side, part, s - 1, k).start()

    def gather_end(l):
        def body(s, _):
            for part in range(2):
                for side in range(2):
                    k = holder(side, s + 1)
                    across(l, 1 - core, side, part, s, k).wait_recv()
                    across(l, core, side, part, s, k).wait_send()
                    ring(l, side, part, s, holder(side, s)).wait_send()
            return 0

        lax.fori_loop(0, n - 1, body, 0)

    def outs(l):
        to = ((gu0_out, d0_out), (gu1_out, d1_out))[l]
        return (
            pltpu.make_async_copy(gu.at[l], to[0], out_sem.at[l, 0]),
            pltpu.make_async_copy(dn.at[l], to[1], out_sem.at[l, 1]),
        )

    for l in range(layers):
        for copy in own(l):
            copy.wait()

    def gather_first(s, _):
        gather_step(0, s)
        return 0

    lax.fori_loop(0, n, gather_first, 0)
    gather_step(1, jnp.int32(0))
    gather_end(0)
    for copy in outs(0):
        copy.start()

    def tile(t, _):
        @pl.when(t < n - 1)
        def _():
            gather_step(1, t + 1)

        x = x_ref[tile_rows(t), :].astype(F32)
        a = (x * scale_of(x)).astype(BF16)
        for c in range(0, ff, CHUNK):
            w = min(CHUNK, ff - c)
            if w == CHUNK:
                g = dot(a, gu[0, 0, :, c : c + w])
                u = dot(a, gu[0, 1, :, c : c + w])
            else:
                both = dot(a, jnp.concatenate([gu[0, 0, :, c : c + w], gu[0, 1, :, c : c + w]], 1))
                g, u = both[:, :w], both[:, w:]
            hid[:, c : c + w] = (g * sigmoid(g) * u).astype(BF16)
        y = dot(hid[...], dn[0]).astype(BF16)
        h_ref[tile_rows(t), :] = (x + y.astype(F32)).astype(BF16)
        return 0

    tiles = x_ref.shape[0] // TILE
    lax.fori_loop(0, tiles, tile, 0)

    def gather_rest(s, _):
        gather_step(1, s)
        return 0

    lax.fori_loop(min(tiles, n - 1) + 1, n, gather_rest, 0)
    gather_end(1)
    for copy in outs(1):
        copy.start()
    for l in range(layers):
        for copy in outs(l):
            copy.wait()


def forward(n, x, gate, up, down):
    tokens, d = x.shape
    layers, rows, ff = gate.shape
    drows = down.shape[1]
    gu, dn = jax.ShapeDtypeStruct((2, d, ff), BF16), jax.ShapeDtypeStruct((n * drows, d), BF16)
    any_, vmem = pl.BlockSpec(memory_space=pl.ANY), pl.BlockSpec(memory_space=pltpu.VMEM)
    sems = pltpu.SemaphoreType.DMA((layers, 2, 2, n - 1))
    return pl.pallas_call(
        functools.partial(forward_kernel, n),
        out_shape=(jax.ShapeDtypeStruct(x.shape, BF16), gu, dn, gu, dn),
        in_specs=[vmem, any_, any_, any_],
        out_specs=(vmem, any_, any_, any_, any_),
        scratch_shapes=[
            pltpu.VMEM((layers, 2, d, ff), BF16),
            pltpu.VMEM((layers, n * drows, d), BF16),
            pltpu.VMEM((TILE, ff), BF16),
            pltpu.SemaphoreType.DMA((layers, 3)),
            pltpu.SemaphoreType.DMA((layers, 2)),
            sems, sems, sems, sems,
        ],
        compiler_params=pltpu.CompilerParams(collective_id=0, has_side_effects=True, vmem_limit_bytes=VMEM_LIMIT),
        name="gather_forward",
    )(x, gate, up, down)


class Ring:
    def __init__(self, n, me, part, out, slots, send, recv):
        self.n, self.me, self.part, self.out, self.slots, self.send, self.recv = n, me, part, out, slots, send, recv

    def copy(self, side, src, s):
        to = lax.rem(self.me + (1 if side == 0 else self.n - 1), self.n)
        return pltpu.make_async_remote_copy(
            src, self.slots.at[side, s], self.send.at[side, s], self.recv.at[side, s], {"dp": to}, MESH
        )

    def owner(self, side, s):
        return lax.rem(self.me + 2 * self.n - 1 - s, self.n) if side == 0 else lax.rem(self.me + 1 + s, self.n)

    def step(self, s):
        n, slots = self.n, self.slots

        @pl.when(s == 0)
        def _():
            for side in range(2):
                self.copy(side, self.part(side, self.owner(side, s)), s).start()

        @pl.when(s > 0)
        def _():
            for side in range(2):
                here = slots.at[side, s - 1]
                self.copy(side, here, s - 1).wait_recv()
                total = here[...].astype(F32) + self.part(side, self.owner(side, s))[...].astype(F32)

                @pl.when(s < n - 1)
                def _():
                    here[...] = total.astype(BF16)
                    self.copy(side, here, s).start()

                @pl.when(s == n - 1)
                def _():
                    self.out(side)[...] = total.astype(BF16)

    def end(self):
        def body(s, _):
            for side in range(2):
                self.copy(side, self.slots.at[side, s], s).wait_send()
            return 0

        lax.fori_loop(0, self.n - 1, body, 0)


def gu_ring(n, me, part, out, bufs):
    rows = part.shape[1] // n
    return Ring(n, me, lambda side, k: part.at[side, pl.ds(pl.multiple_of(k * rows, rows), rows)], lambda side: out.at[side], *bufs)


def down_ring(n, me, part, out, bufs):
    rows, half = part.shape[0] // n, part.shape[1] // 2
    return Ring(
        n, me,
        lambda side, k: part.at[pl.ds(pl.multiple_of(k * rows, 16), rows), pl.ds(side * half, half)],
        lambda side: out.at[:, pl.ds(side * half, half)],
        *bufs,
    )


def ring_scratch(n, rows, columns):
    sems = pltpu.SemaphoreType.DMA((2, n - 1))
    return [pltpu.VMEM((2, n - 1, rows, columns), BF16), sems, sems]


def prepare(tokens, h_ref, dh_ref, a, a_t, dh_t):
    def body(t, _):
        rows = tile_rows(t)
        wide = h_ref[rows, :].astype(F32)
        normed = (wide * scale_of(wide)).astype(BF16)
        a[rows, :] = normed
        a_t[:, rows] = normed.T
        dh_t[:, rows] = dh_ref[rows, :].T
        return 0

    lax.fori_loop(0, tokens // TILE, body, 0)


def backward_chunk(tokens, c, w, refs, place, da, tick):
    dh_ref, gu, dn, a, a_t, dh_t, dn_t, gu_t, acc_g, acc_u, acc_d = refs
    units = pl.ds(c if isinstance(c, int) else pl.multiple_of(c, CHUNK), w)
    dn_t[:, :w] = dn[units, :].T
    if da is not None:
        gu_t[:w] = gu[0, :, units].T
        gu_t[w : 2 * w] = gu[1, :, units].T
    acc_g[...] = jnp.zeros_like(acc_g)
    acc_u[...] = jnp.zeros_like(acc_u)
    acc_d[...] = jnp.zeros_like(acc_d)

    def body(t, _):
        tick(t)
        rows = tile_rows(t)
        at = a[rows, :]
        if w == CHUNK:
            g = dot(at, gu[0, :, units])
            u = dot(at, gu[1, :, units])
        else:
            both = dot(at, jnp.concatenate([gu[0, :, units], gu[1, :, units]], 1))
            g, u = both[:, :w], both[:, w:]
        e = dot(dh_ref[rows, :], dn_t[:, :w]).astype(BF16).astype(F32)
        s = sigmoid(g)
        silu = g * s
        hid = (silu * u).astype(BF16)
        du = (e * silu).astype(BF16)
        dg = (e * u * (s + silu * (1.0 - s))).astype(BF16)
        acc_d[:, :w] += dot(dh_t[:, rows], hid)
        dgu = jnp.concatenate([dg, du], 1)
        if w == CHUNK:
            acc_g[...] += dot(a_t[:, rows], dg)
            acc_u[...] += dot(a_t[:, rows], du)
        else:
            acc_g[...] += dot(a_t[:, rows], dgu)
        if da is not None:
            da[rows, :] += dot(dgu, gu_t[: 2 * w, :])
        return 0

    lax.fori_loop(0, tokens // TILE, body, 0)
    if w == CHUNK:
        place(acc_g[...], acc_u[...], acc_d[...])
    else:
        place(acc_g[:, :w], acc_g[:, w : 2 * w], acc_d[:, :w])


def backward_layer(tokens, ff, refs, parts, part_d, da, tick):
    tiles = tokens // TILE
    first = 0
    for part in parts:
        columns = part.shape[2]

        def placed(c, w, base, part=part):
            def place(g, u, d):
                at = pl.ds(c - base if isinstance(c, int) else pl.multiple_of(c - base, CHUNK), w)
                part[0, :, at] = g.astype(BF16)
                part[1, :, at] = u.astype(BF16)
                part_d[pl.ds(c if isinstance(c, int) else pl.multiple_of(c, CHUNK), w), :] = d.astype(BF16).T

            return place

        whole = columns // CHUNK

        def chunk(j, _, base=first, placed=placed):
            backward_chunk(
                tokens, base + j * CHUNK, CHUNK, refs, placed(base + j * CHUNK, CHUNK, base), da,
                lambda t: tick((base // CHUNK + j) * tiles + t),
            )
            return 0

        lax.fori_loop(0, whole, chunk, 0)
        if columns % CHUNK:
            c = first + whole * CHUNK
            backward_chunk(tokens, c, columns % CHUNK, refs, placed(c, columns % CHUNK, first), da, lambda t, c=c: tick(c // CHUNK * tiles + t))
        first += columns


def at_ticks(k, first, every, ring, n):
    @pl.when((k >= first) & (k < first + n * every) & (lax.rem(k - first + every * 64, every) == 0))
    def _():
        ring.step((k - first) // every)


def last_kernel(n, h_ref, dh_ref, gu, dn, out_h, part_b, part_d, sum_a, a, a_t, dh_t, dn_t, gu_t, acc_g, acc_u, acc_d, da, part_a0, part_a1, *bufs):
    me = lax.axis_index("dp")
    tokens, d = h_ref.shape
    ff = dn.shape[0]
    greet(({"dp": lax.rem(me + 1, n)}, {"dp": lax.rem(me + n - 1, n)}))
    wide = part_a0.shape[2]
    rings = [
        gu_ring(n, me, part_a0, sum_a.at[:, :, pl.ds(0, wide)], bufs[0:3]),
        gu_ring(n, me, part_a1, sum_a.at[:, :, pl.ds(wide, wide)], bufs[3:6]),
    ]
    tiles = tokens // TILE

    def tick(k):
        at_ticks(k, GROUP * tiles, 4, rings[0], n)
        at_ticks(k, 2 * GROUP * tiles + 1, 3, rings[1], n)

    prepare(tokens, h_ref, dh_ref, a, a_t, dh_t)
    da[...] = jnp.zeros_like(da)
    refs = (dh_ref, gu, dn, a, a_t, dh_t, dn_t, gu_t, acc_g, acc_u, acc_d)
    backward_layer(tokens, ff, refs, (part_a0, part_a1, part_b), part_d, da, tick)
    for ring in rings:
        ring.end()

    def finish(t, _):
        rows = tile_rows(t)
        wide = h_ref[rows, :].astype(F32)
        r = scale_of(wide)
        by_a = da[rows, :].astype(BF16).astype(F32)
        by_h = by_a * r - wide * (r * r * r * jnp.mean(by_a * wide, -1, keepdims=True))
        out_h[rows, :] = (dh_ref[rows, :].astype(F32) + by_h.astype(BF16).astype(F32)).astype(BF16)
        return 0

    lax.fori_loop(0, tiles, finish, 0)


def first_kernel(
    n, h_ref, dh_ref, gu, dn, old_b, old_d, sum_old_b, sum_old_d, sum_a, sum_b, sum_d,
    a, a_t, dh_t, dn_t, acc_g, acc_u, acc_d, part_a0, part_a1, part_b, part_d, *bufs,
):
    me = lax.axis_index("dp")
    tokens, d = h_ref.shape
    ff = dn.shape[0]
    greet(({"dp": lax.rem(me + 1, n)}, {"dp": lax.rem(me + n - 1, n)}))
    wide = part_a0.shape[2]
    old = [down_ring(n, me, old_d, sum_old_d, bufs[0:3]), gu_ring(n, me, old_b, sum_old_b, bufs[3:6])]
    groups = [
        gu_ring(n, me, part_a0, sum_a.at[:, :, pl.ds(0, wide)], bufs[6:9]),
        gu_ring(n, me, part_a1, sum_a.at[:, :, pl.ds(wide, wide)], bufs[9:12]),
    ]
    tail = [down_ring(n, me, part_d, sum_d, bufs[12:15]), gu_ring(n, me, part_b, sum_b, bufs[15:18])]
    tiles = tokens // TILE

    def tick(k):
        at_ticks(k, 0, 4, old[0], n)
        at_ticks(k, 2, 4, old[1], n)
        at_ticks(k, GROUP * tiles + 1, 4, groups[0], n)
        at_ticks(k, 2 * GROUP * tiles, 3, groups[1], n)

    prepare(tokens, h_ref, dh_ref, a, a_t, dh_t)
    refs = (dh_ref, gu, dn, a, a_t, dh_t, dn_t, None, acc_g, acc_u, acc_d)
    backward_layer(tokens, ff, refs, (part_a0, part_a1, part_b), part_d, None, tick)

    def rest(s, _):
        for ring in tail:
            ring.step(s)
        return 0

    lax.fori_loop(0, n, rest, 0)
    for ring in old + groups + tail:
        ring.end()


def work_scratch(tokens, d):
    return [
        pltpu.VMEM((tokens, d), BF16),
        pltpu.VMEM((d, tokens), BF16),
        pltpu.VMEM((d, tokens), BF16),
        pltpu.VMEM((d, CHUNK), BF16),
    ]


def sums_scratch(d):
    return [pltpu.VMEM((d, CHUNK), F32)] * 3


def backward_last(n, h, dh, gu, dn):
    tokens, d = h.shape
    ff = dn.shape[0]
    wide, rest = GROUP * CHUNK, ff - 2 * GROUP * CHUNK
    vmem = pl.BlockSpec(memory_space=pltpu.VMEM)
    return pl.pallas_call(
        functools.partial(last_kernel, n),
        out_shape=(
            jax.ShapeDtypeStruct((tokens, d), BF16),
            jax.ShapeDtypeStruct((2, d, rest), BF16),
            jax.ShapeDtypeStruct((ff, d), BF16),
            jax.ShapeDtypeStruct((2, d // n, 2 * wide), BF16),
        ),
        in_specs=[vmem] * 4,
        out_specs=(vmem,) * 4,
        scratch_shapes=work_scratch(tokens, d)
        + [pltpu.VMEM((2 * CHUNK, d), BF16)]
        + sums_scratch(d)
        + [pltpu.VMEM((tokens, d), F32)]
        + [pltpu.VMEM((2, d, wide), BF16)] * 2
        + ring_scratch(n, d // n, wide)
        + ring_scratch(n, d // n, wide),
        compiler_params=pltpu.CompilerParams(collective_id=1, has_side_effects=True, vmem_limit_bytes=VMEM_LIMIT),
        name="layer1",
    )(h, dh, gu, dn)


def backward_first(n, h, dh, gu, dn, old_b, old_d):
    tokens, d = h.shape
    ff = dn.shape[0]
    wide, rest = GROUP * CHUNK, ff - 2 * GROUP * CHUNK
    vmem = pl.BlockSpec(memory_space=pltpu.VMEM)
    b, dd = jax.ShapeDtypeStruct((2, d // n, rest), BF16), jax.ShapeDtypeStruct((ff // n, d), BF16)
    return pl.pallas_call(
        functools.partial(first_kernel, n),
        out_shape=(b, dd, jax.ShapeDtypeStruct((2, d // n, 2 * wide), BF16), b, dd),
        in_specs=[vmem] * 6,
        out_specs=(vmem,) * 5,
        scratch_shapes=work_scratch(tokens, d)
        + sums_scratch(d)
        + [pltpu.VMEM((2, d, wide), BF16)] * 2
        + [pltpu.VMEM((2, d, rest), BF16), pltpu.VMEM((ff, d), BF16)]
        + ring_scratch(n, ff // n, d // 2)
        + ring_scratch(n, d // n, rest)
        + ring_scratch(n, d // n, wide)
        + ring_scratch(n, d // n, wide)
        + ring_scratch(n, ff // n, d // 2)
        + ring_scratch(n, d // n, rest),
        compiler_params=pltpu.CompilerParams(collective_id=2, has_side_effects=True, vmem_limit_bytes=VMEM_LIMIT),
        name="layer0",
    )(h, dh, gu, dn, old_b, old_d)


def solution(mesh):
    n = mesh.shape["dp"]

    def step(x, dy, *arrays):
        weights, m, v = (arrays[i : i + 3] for i in (0, 3, 6))
        h1, gu0, d0, gu1, d1 = forward(n, x[0], *weights)
        by_h1, part_b1, part_d1, sum_a1 = backward_last(n, h1, dy[0], gu1, d1)
        sum_b1, sum_d1, sum_a0, sum_b0, sum_d0 = backward_first(n, x[0], by_h1, gu0, d0, part_b1, part_d1)
        gu_sums = [jnp.concatenate(pair, -1) for pair in ((sum_a0, sum_b0), (sum_a1, sum_b1))]
        gradients = [jnp.stack([s[i] for s in gu_sums]).astype(F32) for i in range(2)]
        gradients.append(jnp.stack([sum_d0, sum_d1]).astype(F32))
        new = [adamw(w.astype(F32), m, v, g) for w, m, v, g in zip(weights, m, v, gradients, strict=True)]
        return tuple(one[which] for which in range(3) for one in new)

    states, cut = P(("rep", "dp"), None, None), P(None, "dp", None)
    return jax.shard_map(
        step,
        mesh=mesh,
        in_specs=(states, states) + (cut,) * 9,
        out_specs=(P("rep", "dp", None),) * 9,
        check_vma=False,
    )
```

time: 571 us -> 311 us (0.54); the launches traced: 563 us -> 311 us
  Pallas kernels: 0 us -> 302 us
  matrix products: 283 us -> 0 us
  waiting for transfers between devices: 230 us -> 0 us
  local copies, waits for them, and re-layouts: 19.1 us -> 3.23 us
  between operations: 14.9 us -> 0.82 us
  other arithmetic: 15.2 us -> 4.7 us
    pallas_call x0 -> x3, Pallas kernels: none -> 302 us  [the longest x1 117 us: backward_first(): pl.pallas_call(functools.partial(first_kernel, n), out_shape=(b, dd, jax....]
    dot_general x15 -> x0, matrix products: 283 us -> none  [the longest x5 106 us: layer(): gate = jnp.dot(a, w['w_gate'], preferred_element_type=jnp.float32)]
    all_gather x6 -> x0, waiting for transfers between devices: 120 us -> none  [fetched(): lax.all_gather(w[number], 'dp', axis=0, tiled=True)]
    reduce_scatter x6 -> x0, waiting for transfers between devices: 108 us -> none  [step(): lax.psum_scatter(by_w[name], 'dp', scatter_dimension=0, tiled=True)]
    unnamed x32 -> x26, local copies, waits for them, and re-layouts: 13.6 us -> 1.98 us
  transfers between devices with their start and end apart: 12 -> 0, of which waited for: 9 -> 0; matrix products, arithmetic and copies ran while one was open for 46% -> 0% of each run, Pallas kernels for 0% -> 0%
where the time goes in v1:
time: 311 us
  Pallas kernels  302 us (97%)
  other arithmetic  4.7 us (2%)
  local copies, waits for them, and re-layouts  3.23 us (1%)
    pallas_call x1, Pallas kernels, backward_first(): pl.pallas_call(functools.partial(first_kernel, n), out_shape=(b, dd, jax....  117 us
    pallas_call x1, Pallas kernels, backward_last(): pl.pallas_call(functools.partial(last_kernel, n), out_shape=(jax.ShapeDty...  98.1 us
    pallas_call x1, Pallas kernels, forward(): pl.pallas_call(functools.partial(forward_kernel, n), out_shape=(jax.Shape...  87 us

profile of v1, /device:TPU:22, one launch (start us, length us, event | category | flops | bytes accessed | tf_op | source)
XLA Modules:
  0.0 311.1 jit_solution(18049390352105178359)
XLA Ops:
  0.6 87.0 %gather_forward.1 = (bf16[4096,512]{1,0:T(8,128)(2,1)}, bf16[2,512,1664]{2,1,0:T(8,128)(2,1)}, bf16[1664,512]{1,0:T(8,128)(2,1)}, bf16[2,512,1664]{2,1,0:T(8,128)(2,1)}, bf16[1664,512]{1,0:T(8,128)(2,1)}) custom-call(bf16[4096,512]{1,0:T(8,128)(2,1)} %bitcast.4, bf16[2,64,1664]{2,1,0:T(8,128)(2,1)} %gate_ref.1, bf16[2,64,1664]{2,1,0:T(8,128)(2,1)} %up_ref.1, ...), custom_call_target="tpu_custom_call" | custom-call | tf_op jit(solution)/shard_map/gather_forward/pallas_call | solution.py:190
  87.7 98.1 %layer1.1 = (bf16[4096,512]{1,0:T(8,128)(2,1)}, bf16[2,512,640]{2,1,0:T(8,128)(2,1)}, bf16[1664,512]{1,0:T(8,128)(2,1)}, bf16[2,64,1024]{2,1,0:T(8,128)(2,1)}) custom-call(bf16[4096,512]{1,0:T(8,128)(2,1)} %get-tuple-element.23.h_ref, bf16[4096,512]{1,0:T(8,128)(2,1)} %bitcast.6, bf16[2,512,1664]{2,1,0:T(8,128)(2,1)} %get-tuple-element.24.gu, ...), custom_call_target="tpu_custom_call" | custom-call | tf_op jit(solution)/shard_map/layer1/pallas_call | solution.py:459
  185.8 0.0 copy-start.9
  185.8 117.2 %layer0.1 = (bf16[2,64,640]{2,1,0:T(8,128)(2,1)}, bf16[208,512]{1,0:T(8,128)(2,1)}, bf16[2,64,1024]{2,1,0:T(8,128)(2,1)}, bf16[2,64,640]{2,1,0:T(8,128)(2,1)}, bf16[208,512]{1,0:T(8,128)(2,1)}) custom-call(bf16[4096,512]{1,0:T(8,128)(2,1)} %bitcast.5, bf16[4096,512]{1,0:T(8,128)(2,1)} %get-tuple-element.26.dh_ref, ...), custom_call_target="tpu_custom_call" | custom-call | tf_op jit(solution)/shard_map/layer0/pallas_call | solution.py:487
  303.1 0.0 copy-start
  303.1 0.0 copy-start.3
  303.1 0.0 copy-start.4
  303.1 1.1 constant_dynamic-update-slice_fusion.1
  304.2 0.0 copy-done.9
  304.3 0.0 copy-start.1
  304.3 0.0 copy-start.5
  304.3 0.0 copy-start.6
  304.3 1.2 constant_dynamic-update-slice_fusion
  305.6 0.0 copy-done
  305.6 0.0 copy-done.3
  305.6 0.0 copy-done.4
  305.6 1.6 fusion.6
  307.2 0.0 copy-start.2
  307.2 0.0 copy-start.7
  307.2 0.0 copy-start.8
  307.2 0.0 copy-start.10
  307.2 0.0 copy-start.11
  307.2 0.0 copy-done.1
  307.2 0.0 copy-done.5
  307.2 0.0 copy-done.6
  307.2 1.6 fusion.2
  308.8 0.0 copy-done.2
  308.8 0.1 copy-done.7
  308.8 0.6 copy-done.8
  309.5 0.0 copy-done.10
  309.5 0.1 copy-done.11
  309.6 1.6 fusion.10
  (3 shorter events, 0.1 us)
Async XLA Ops:
  185.8 118.4 %copy-start.9 = (bf16[2,64,1024]{2,1,0:T(8,128)(2,1)S(1)}, bf16[2,64,1024]{2,1,0:T(8,128)(2,1)}, u32[]{:S(2)}) copy-start(bf16[2,64,1024]{2,1,0:T(8,128)(2,1)} %get-tuple-element.33) | copy-start | bytes 786436
  303.1 2.5 copy-start
  303.1 2.5 copy-start.3
  303.1 2.5 copy-start.4
  304.3 2.9 copy-start.1
  304.3 2.9 copy-start.5
  304.3 2.9 copy-start.6
  307.2 1.6 copy-start.2
  307.2 1.7 copy-start.7
  307.2 2.3 copy-start.8
  307.2 2.3 copy-start.10
  307.2 2.4 copy-start.11

commit v2 on v1

v2 whole, which is shorter than its diff:
```python
import functools

import jax
import jax.numpy as jnp
from jax import lax
from jax.experimental import pallas as pl
from jax.experimental.pallas import tpu as pltpu
from jax.sharding import PartitionSpec as P

BF16, F32 = jnp.bfloat16, jnp.float32
MESH = pl.DeviceIdType.MESH
TILE = 512
CHUNK = 256
PIECES = 4
EARLY = 5
VMEM_LIMIT = 63 * 1024 * 1024


def dot(a, b):
    return jnp.dot(a, b, preferred_element_type=F32)


def scale_of(wide):
    return lax.rsqrt(jnp.mean(wide * wide, -1, keepdims=True) + 1e-6)


def sigmoid(g):
    return 0.5 * jnp.tanh(0.5 * g) + 0.5


def adamw(w, m, v, g):
    m = 0.9 * m + 0.1 * g
    v = 0.95 * v + 0.05 * g * g
    step = m * lax.rsqrt(v + 1e-8) + 0.1 * w
    return (w - 0.02 * step).astype(BF16), m, v


def tile_rows(t):
    return pl.ds(pl.multiple_of(t * TILE, TILE), TILE)


def greet(others):
    barrier = pltpu.get_barrier_semaphore()
    for other in others:
        pl.semaphore_signal(barrier, inc=1, device_id=other, device_id_type=MESH)
    pl.semaphore_wait(barrier, len(others))


def forward_kernel(
    n, x_ref, gate_ref, up_ref, down_ref, h_ref, gu0_out, d0_out, gu1_out, d1_out,
    gu, dn, hid, own_sem, out_sem, send_sem, recv_sem, psend_sem, precv_sem,
):
    me = lax.axis_index("dp")
    rep = lax.axis_index("rep")
    core = lax.rem(rep, 2)
    right, left = {"dp": lax.rem(me + 1, n)}, {"dp": lax.rem(me + n - 1, n)}
    partner = {"rep": rep + 1 - 2 * core}
    layers, rows, ff = gate_ref.shape
    drows, d = down_ref.shape[1:]
    half, quarter = d // 2, d // 4
    tiles = x_ref.shape[0] // TILE

    def own(l):
        mine = pl.ds(pl.multiple_of(me * rows, rows), rows)
        down = pl.ds(pl.multiple_of(me * drows, 16), drows)
        return (
            pltpu.make_async_copy(gate_ref.at[l], gu.at[l, 0, mine], own_sem.at[l, 0]),
            pltpu.make_async_copy(up_ref.at[l], gu.at[l, 1, mine], own_sem.at[l, 1]),
            pltpu.make_async_copy(down_ref.at[l], dn.at[l, down], own_sem.at[l, 2]),
        )

    for l in range(layers):
        for copy in own(l):
            copy.start()
    greet((right, left, partner))

    def piece(l, c, part, k):
        if part < 2:
            start = pl.multiple_of(k * rows + part * (rows // 2), rows // 2)
            return gu.at[l, c, pl.ds(start, rows // 2)]
        start = pl.multiple_of(k * drows, 16)
        return dn.at[l, pl.ds(start, drows), pl.ds(pl.multiple_of(c * half + (part - 2) * quarter, quarter), quarter)]

    def hops(side, part):
        return n // 2 if side == part % 2 else n - 1 - n // 2

    def ring(l, side, part, s, k):
        ref = piece(l, core, part, k)
        return pltpu.make_async_remote_copy(
            ref, ref, send_sem.at[l, side, part, s], recv_sem.at[l, side, part, s], (right, left)[side], MESH
        )

    def across(l, c, side, part, s, k):
        ref = piece(l, c, part, k)
        return pltpu.make_async_remote_copy(
            ref, ref, psend_sem.at[l, side, part, s], precv_sem.at[l, side, part, s], partner, MESH
        )

    def holder(side, s):
        return lax.rem(me + n - s, n) if side == 0 else lax.rem(me + s, n)

    def gather_step(l, s):
        for part in range(PIECES):
            for side in range(2):
                k, last = holder(side, s), hops(side, part)

                @pl.when((s > 0) & (s <= last))
                def _():
                    ring(l, side, part, s - 1, k).wait_recv()

                @pl.when(s < last)
                def _():
                    ring(l, side, part, s, k).start()

                @pl.when((s > 0) & (s <= last))
                def _():
                    across(l, core, side, part, s - 1, k).start()

    def gather_end(l):
        def body(s, _):
            for part in range(PIECES):
                for side in range(2):

                    @pl.when(s < hops(side, part))
                    def _():
                        k = holder(side, s + 1)
                        across(l, 1 - core, side, part, s, k).wait_recv()
                        across(l, core, side, part, s, k).wait_send()
                        ring(l, side, part, s, holder(side, s)).wait_send()

            return 0

        lax.fori_loop(0, n // 2, body, 0)

    def outs(l):
        to = ((gu0_out, d0_out), (gu1_out, d1_out))[l]
        return (
            pltpu.make_async_copy(gu.at[l], to[0], out_sem.at[l, 0]),
            pltpu.make_async_copy(dn.at[l], to[1], out_sem.at[l, 1]),
        )

    for l in range(layers):
        for copy in own(l):
            copy.wait()

    def gather_first(s, _):
        gather_step(0, s)

        @pl.when(s == n // 4)
        def _():
            gather_step(1, s - n // 4)

        return 0

    lax.fori_loop(0, n // 2 + 1, gather_first, 0)
    gather_end(0)
    for copy in outs(0):
        copy.start()

    def tile(t, _):
        @pl.when(lax.rem(t * (n // 2), tiles) < n // 2)
        def _():
            gather_step(1, 1 + t * (n // 2) // tiles)

        x = x_ref[tile_rows(t), :].astype(F32)
        a = (x * scale_of(x)).astype(BF16)
        for c in range(0, ff, CHUNK):
            w = min(CHUNK, ff - c)
            if w == CHUNK:
                g = dot(a, gu[0, 0, :, c : c + w])
                u = dot(a, gu[0, 1, :, c : c + w])
            else:
                both = dot(a, jnp.concatenate([gu[0, 0, :, c : c + w], gu[0, 1, :, c : c + w]], 1))
                g, u = both[:, :w], both[:, w:]
            hid[:, c : c + w] = (g * sigmoid(g) * u).astype(BF16)
        y = dot(hid[...], dn[0]).astype(BF16)
        h_ref[tile_rows(t), :] = (x + y.astype(F32)).astype(BF16)
        return 0

    lax.fori_loop(0, tiles, tile, 0)
    gather_end(1)
    for copy in outs(1):
        copy.start()
    for l in range(layers):
        for copy in outs(l):
            copy.wait()


def forward(n, x, gate, up, down):
    tokens, d = x.shape
    layers, rows, ff = gate.shape
    drows = down.shape[1]
    gu, dn = jax.ShapeDtypeStruct((2, d, ff), BF16), jax.ShapeDtypeStruct((n * drows, d), BF16)
    any_, vmem = pl.BlockSpec(memory_space=pl.ANY), pl.BlockSpec(memory_space=pltpu.VMEM)
    sems = pltpu.SemaphoreType.DMA((layers, 2, PIECES, n // 2))
    return pl.pallas_call(
        functools.partial(forward_kernel, n),
        out_shape=(jax.ShapeDtypeStruct(x.shape, BF16), gu, dn, gu, dn),
        in_specs=[vmem, any_, any_, any_],
        out_specs=(vmem, any_, any_, any_, any_),
        scratch_shapes=[
            pltpu.VMEM((layers, 2, d, ff), BF16),
            pltpu.VMEM((layers, n * drows, d), BF16),
            pltpu.VMEM((TILE, ff), BF16),
            pltpu.SemaphoreType.DMA((layers, 3)),
            pltpu.SemaphoreType.DMA((layers, 2)),
            sems, sems, sems, sems,
        ],
        compiler_params=pltpu.CompilerParams(collective_id=0, has_side_effects=True, vmem_limit_bytes=VMEM_LIMIT),
        name="gather_forward",
    )(x, gate, up, down)


class Rings:
    def __init__(self, n, me, w, gu, dn, base, out_gu, out_dn, bufs):
        self.n, self.me, self.w, self.gu, self.dn, self.base, self.out_gu, self.out_dn = n, me, w, gu, dn, base, out_gu, out_dn
        self.bufs = (bufs[0:3], bufs[3:6])
        self.rows, self.half = gu.shape[1] // n, dn.shape[1] // 2
        self.far = n // 2
        self.actions = self.far + 1

    def hops(self, p, side):
        return self.far if side == p else self.n - 1 - self.far

    def part(self, kind, j, p, k):
        first = self.base + j * self.w
        if kind == 0:
            first = first if isinstance(first, int) else pl.multiple_of(first, self.w)
            return self.gu.at[p, pl.ds(pl.multiple_of(k * self.rows, self.rows), self.rows), pl.ds(first, self.w)]
        share = self.w // self.n
        return self.dn.at[pl.ds(pl.multiple_of(first + k * share, share), share), pl.ds(p * self.half, self.half)]

    def copy(self, kind, j, p, side, src, s):
        slots, send, recv = self.bufs[kind]
        at = s if side == 0 else self.hops(p, 0) + s
        to = lax.rem(self.me + (1 if side == 0 else self.n - 1), self.n)
        return pltpu.make_async_remote_copy(src, slots.at[j, p, at], send.at[j, p, at], recv.at[j, p, at], {"dp": to}, MESH)

    def slot(self, kind, j, p, side, s):
        return self.bufs[kind][0].at[j, p, s if side == 0 else self.hops(p, 0) + s]

    def step(self, j, s):
        n, me = self.n, self.me

        def whose(p, side, s):
            left = self.hops(p, side) - s
            return lax.rem(me + left, n) if side == 0 else lax.rem(me + n - left, n)

        every = [(kind, p, side) for kind in range(2) for p in range(2) for side in range(2)]

        @pl.when(s == 0)
        def _():
            for kind, p, side in every:
                self.copy(kind, j, p, side, self.part(kind, j, p, whose(p, side, 0)), 0).start()

        @pl.when((s > 0) & (s < self.far))
        def _():
            for kind, p, side in every:

                @pl.when(s < self.hops(p, side))
                def _():
                    here = self.slot(kind, j, p, side, s - 1)
                    self.copy(kind, j, p, side, here, s - 1).wait_recv()
                    term = self.part(kind, j, p, whose(p, side, s))[...]
                    here[...] = (here[...].astype(F32) + term.astype(F32)).astype(BF16)
                    self.copy(kind, j, p, side, here, s).start()

        @pl.when(s == self.far)
        def _():
            for kind in range(2):
                for p in range(2):
                    total = self.part(kind, j, p, me)[...].astype(F32)
                    for side in range(2):
                        here = self.slot(kind, j, p, side, self.hops(p, side) - 1)
                        self.copy(kind, j, p, side, here, self.hops(p, side) - 1).wait_recv()
                        total += here[...].astype(F32)
                    (self.out_gu(p, j) if kind == 0 else self.out_dn(p, j))[...] = total.astype(BF16)

    def end(self, count):
        def body(j, _):
            for kind in range(2):
                for p in range(2):
                    for side in range(2):
                        for s in range(self.hops(p, side)):
                            self.copy(kind, j, p, side, self.slot(kind, j, p, side, s), s).wait_send()
            return 0

        lax.fori_loop(0, count, body, 0)


def ring_scratch(n, count, w, d):
    sems = pltpu.SemaphoreType.DMA((count, 2, n - 1))
    return [
        pltpu.VMEM((count, 2, n - 1, d // n, w), BF16), sems, sems,
        pltpu.VMEM((count, 2, n - 1, w // n, d // 2), BF16), sems, sems,
    ]


def columns(ref, first, w):
    return lambda side, j: ref[side].at[:, pl.ds(first + j * w if isinstance(j, int) else pl.multiple_of(first + j * w, w), w)]


def shares(ref, first, n, w):
    half = ref.shape[1] // 2
    return lambda side, j: ref.at[pl.ds(pl.multiple_of(first + j * (w // n), w // n), w // n), pl.ds(side * half, half)]


def rotate3(rings, k, count, tiles):
    for more in (0, 3):
        j = lax.rem(2 * k + 2, 3) + more
        since = k - tiles * (j + 1)

        @pl.when((j < count) & (since >= 0) & (since < 3 * rings.actions))
        def _():
            rings.step(j, since // 3)


def rotate4(rings, k, count, tiles):
    for more in (0, 4):
        j = lax.rem(k, 4) + more
        since = k - tiles * (j + 1) - lax.rem(k, 4)

        @pl.when((j < count) & (since >= 0) & (since < 4 * rings.actions))
        def _():
            rings.step(j, since // 4)


class Handover:
    def __init__(self, n, me, ff, summed, to, send, recv):
        self.n, self.me, self.summed, self.to, self.send, self.recv = n, me, summed, to, send, recv
        self.units, self.per = ff // 16 // n, CHUNK // n // 16
        self.whole = ff // CHUNK * (CHUNK // 16)

    def copy(self, i):
        n, me, per = self.n, self.me, self.per
        whole = ff_unit = (i // per) * (n * per) + me * per + i % per
        if i * n * 16 >= self.whole * 16:
            left = self.units - self.whole // n
            ff_unit = self.whole + me * left + (i - self.whole // n)
        del whole
        owner, slot = ff_unit // self.units, lax.rem(ff_unit, self.units)
        src, dst = self.summed.at[pl.ds(16 * i, 16)], self.to.at[slot]
        return owner, slot, pltpu.make_async_remote_copy(src, dst, self.send.at[i], self.recv.at[slot], {"dp": owner}, MESH)

    def start(self):
        for i in range(self.units):
            owner, slot, copy = self.copy(i)

            @pl.when(owner == self.me)
            def _():
                self.to[slot] = self.summed[16 * i : 16 * i + 16, :]

            @pl.when(owner != self.me)
            def _():
                copy.start()

    def end(self):
        for i in range(self.units):
            owner, _, copy = self.copy(i)

            @pl.when(owner != self.me)
            def _():
                copy.wait_send()

        def body(slot, _):
            unit = self.units * self.me + slot
            left = self.units - self.whole // self.n
            source = jnp.where(unit < self.whole, lax.rem(unit, self.n * self.per) // self.per, (unit - self.whole) // left)

            @pl.when(source != self.me)
            def _():
                ref = self.to.at[slot]
                pltpu.make_async_remote_copy(ref, ref, self.send.at[0], self.recv.at[slot], {"dp": source}, MESH).wait_recv()

            return 0

        lax.fori_loop(0, self.units, body, 0)


def prepare(tokens, h_ref, dh_ref, a, a_t, dh_t):
    def body(t, _):
        rows = tile_rows(t)
        wide = h_ref[rows, :].astype(F32)
        normed = (wide * scale_of(wide)).astype(BF16)
        a[rows, :] = normed
        a_t[:, rows] = normed.T
        dh_t[:, rows] = dh_ref[rows, :].T
        return 0

    lax.fori_loop(0, tokens // TILE, body, 0)


def backward_chunk(tokens, c, w, refs, place, da, tick):
    dh_ref, gu, dn, a, a_t, dh_t, dn_t, gu_t, acc_g, acc_u, acc_d = refs
    units = pl.ds(c if isinstance(c, int) else pl.multiple_of(c, CHUNK), w)
    dn_t[:, :w] = dn[units, :].T
    if da is not None:
        gu_t[:w] = gu[0, :, units].T
        gu_t[w : 2 * w] = gu[1, :, units].T
    acc_g[...] = jnp.zeros_like(acc_g)
    acc_u[...] = jnp.zeros_like(acc_u)
    acc_d[...] = jnp.zeros_like(acc_d)

    def body(t, _):
        tick(t)
        rows = tile_rows(t)
        at = a[rows, :]
        if w == CHUNK:
            g = dot(at, gu[0, :, units])
            u = dot(at, gu[1, :, units])
        else:
            both = dot(at, jnp.concatenate([gu[0, :, units], gu[1, :, units]], 1))
            g, u = both[:, :w], both[:, w:]
        e = dot(dh_ref[rows, :], dn_t[:, :w]).astype(BF16).astype(F32)
        s = sigmoid(g)
        silu = g * s
        hid = (silu * u).astype(BF16)
        du = (e * silu).astype(BF16)
        dg = (e * u * (s + silu * (1.0 - s))).astype(BF16)
        acc_d[:, :w] += dot(dh_t[:, rows], hid)
        dgu = jnp.concatenate([dg, du], 1)
        if w == CHUNK:
            acc_g[...] += dot(a_t[:, rows], dg)
            acc_u[...] += dot(a_t[:, rows], du)
        else:
            acc_g[...] += dot(a_t[:, rows], dgu)
        if da is not None:
            da[rows, :] += dot(dgu, gu_t[: 2 * w, :])
        return 0

    lax.fori_loop(0, tokens // TILE, body, 0)
    if w == CHUNK:
        place(acc_g[...], acc_u[...], acc_d[...])
    else:
        place(acc_g[:, :w], acc_g[:, w : 2 * w], acc_d[:, :w])


def backward_layer(tokens, refs, place, ff, da, tick):
    tiles = tokens // TILE
    whole = ff // CHUNK

    def chunk(j, _):
        c = pl.multiple_of(j * CHUNK, CHUNK)
        backward_chunk(tokens, c, CHUNK, refs, place(c, CHUNK), da, lambda t: tick(j * tiles + t))
        return 0

    lax.fori_loop(0, whole, chunk, 0)
    if ff % CHUNK:
        backward_chunk(tokens, whole * CHUNK, ff % CHUNK, refs, place(whole * CHUNK, ff % CHUNK), da, lambda t: tick(whole * tiles + t))


def placer(gu_part, dn_part):
    def place(c, w):
        def put(g, u, d):
            gu_part[0, :, pl.ds(c, w)] = g.astype(BF16)
            gu_part[1, :, pl.ds(c, w)] = u.astype(BF16)
            dn_part[pl.ds(c, w), :] = d.astype(BF16).T

        return put

    return place


def last_kernel(
    n, early, h_ref, dh_ref, gu, dn, out_h, out_gu, out_dn, sum_g, sum_u, sum_d,
    a, a_t, dh_t, dn_t, gu_t, acc_g, acc_u, acc_d, da, gu_part, dn_part, *bufs,
):
    me = lax.axis_index("dp")
    tokens, d = h_ref.shape
    ff = dn.shape[0]
    greet(({"dp": lax.rem(me + 1, n)}, {"dp": lax.rem(me + n - 1, n)}))
    rings = Rings(n, me, CHUNK, gu_part, dn_part, 0, columns((sum_g, sum_u), 0, CHUNK), shares(sum_d, 0, n, CHUNK), bufs)
    tiles = tokens // TILE
    prepare(tokens, h_ref, dh_ref, a, a_t, dh_t)
    da[...] = jnp.zeros_like(da)
    refs = (dh_ref, gu, dn, a, a_t, dh_t, dn_t, gu_t, acc_g, acc_u, acc_d)
    backward_layer(tokens, refs, placer(gu_part, dn_part), ff, da, lambda k: rotate3(rings, k, early, tiles))
    out_gu[...] = gu_part[:, :, early * CHUNK :]
    out_dn[...] = dn_part[early * CHUNK :, :]

    def finish(t, _):
        rows = tile_rows(t)
        wide = h_ref[rows, :].astype(F32)
        r = scale_of(wide)
        by_a = da[rows, :].astype(BF16).astype(F32)
        by_h = by_a * r - wide * (r * r * r * jnp.mean(by_a * wide, -1, keepdims=True))
        out_h[rows, :] = (dh_ref[rows, :].astype(F32) + by_h.astype(BF16).astype(F32)).astype(BF16)
        return 0

    lax.fori_loop(0, tiles, finish, 0)
    rings.end(early)


def first_kernel(
    n, early, h_ref, dh_ref, gu, dn, old_gu, old_dn, old_sum_g, old_sum_u, old_sum_d, sum_g, sum_u, sum_d,
    a, a_t, dh_t, dn_t, acc_g, acc_u, acc_d, gu_part, dn_part, summed, old_summed, send, recv, old_send, old_recv, *bufs,
):
    me = lax.axis_index("dp")
    tokens, d = h_ref.shape
    ff = dn.shape[0]
    whole, left = ff // CHUNK, ff % CHUNK
    share = CHUNK // n
    barrier = pltpu.get_barrier_semaphore()
    for other in range(1, n):
        pl.semaphore_signal(barrier, inc=1, device_id={"dp": lax.rem(me + other, n)}, device_id_type=MESH)
    pl.semaphore_wait(barrier, n - 1)
    old_g, old_u, new_g, new_u = sum_g.at[1], sum_u.at[1], sum_g.at[0], sum_u.at[0]
    old = Rings(
        n, me, CHUNK, old_gu, old_dn, 0, columns((old_g, old_u), early * CHUNK, CHUNK), shares(old_summed, early * share, n, CHUNK), bufs[0:6]
    )
    old_left = Rings(
        n, me, left, old_gu, old_dn, (whole - early) * CHUNK, columns((old_g, old_u), whole * CHUNK, left), shares(old_summed, whole * share, n, left), bufs[6:12]
    )
    new = Rings(n, me, CHUNK, gu_part, dn_part, 0, columns((new_g, new_u), 0, CHUNK), shares(summed, 0, n, CHUNK), bufs[12:18])
    new_left = Rings(
        n, me, left, gu_part, dn_part, whole * CHUNK, columns((new_g, new_u), whole * CHUNK, left), shares(summed, whole * share, n, left), bufs[18:24]
    )
    tiles = tokens // TILE

    def tick(k):
        slot, s = lax.rem(k, 4), k // 4

        @pl.when((s < old.actions) & (slot < whole - early))
        def _():
            old.step(slot, s)

        @pl.when((s < old.actions) & (slot == 2))
        def _():
            old_left.step(0, s)

        rotate4(new, k, whole, tiles)

    prepare(tokens, h_ref, dh_ref, a, a_t, dh_t)
    ready = early * CHUNK
    sum_g[1, :, :ready] = old_sum_g[...]
    sum_u[1, :, :ready] = old_sum_u[...]
    old_summed[: early * share, :] = old_sum_d[...]
    refs = (dh_ref, gu, dn, a, a_t, dh_t, dn_t, None, acc_g, acc_u, acc_d)
    backward_layer(tokens, refs, placer(gu_part, dn_part), ff, None, tick)
    old_over = Handover(n, me, ff, old_summed, sum_d.at[1], old_send, old_recv)
    over = Handover(n, me, ff, summed, sum_d.at[0], send, recv)
    total = (whole + 1) * tiles

    def rest(i, _):
        @pl.when(lax.rem(i, 4) == 2)
        def _():
            new_left.step(0, i // 4)

        rotate4(new, total + i, whole, tiles)
        return 0

    lax.fori_loop(0, 4, rest, 0)
    old_over.start()
    lax.fori_loop(4, 4 * new.actions, rest, 0)
    over.start()
    old.end(whole - early)
    old_left.end(1)
    new.end(whole)
    new_left.end(1)
    old_over.end()
    over.end()


def work_scratch(tokens, d):
    return [
        pltpu.VMEM((tokens, d), BF16),
        pltpu.VMEM((d, tokens), BF16),
        pltpu.VMEM((d, tokens), BF16),
        pltpu.VMEM((d, CHUNK), BF16),
    ]


def sums_scratch(d):
    return [pltpu.VMEM((d, CHUNK), F32)] * 3


def backward_last(n, early, h, dh, gu, dn):
    tokens, d = h.shape
    ff = dn.shape[0]
    ready = early * CHUNK
    vmem = pl.BlockSpec(memory_space=pltpu.VMEM)
    gu_sum = jax.ShapeDtypeStruct((d // n, ready), BF16)
    return pl.pallas_call(
        functools.partial(last_kernel, n, early),
        out_shape=(
            jax.ShapeDtypeStruct((tokens, d), BF16),
            jax.ShapeDtypeStruct((2, d, ff - ready), BF16),
            jax.ShapeDtypeStruct((ff - ready, d), BF16),
            gu_sum, gu_sum, jax.ShapeDtypeStruct((ready // n, d), BF16),
        ),
        in_specs=[vmem] * 4,
        out_specs=(vmem,) * 6,
        scratch_shapes=work_scratch(tokens, d)
        + [pltpu.VMEM((2 * CHUNK, d), BF16)]
        + sums_scratch(d)
        + [pltpu.VMEM((tokens, d), F32), pltpu.VMEM((2, d, ff), BF16), pltpu.VMEM((ff, d), BF16)]
        + ring_scratch(n, early, CHUNK, d),
        compiler_params=pltpu.CompilerParams(collective_id=1, has_side_effects=True, vmem_limit_bytes=VMEM_LIMIT),
        name="layer1",
    )(h, dh, gu, dn)


def backward_first(n, early, h, dh, gu, dn, *old):
    tokens, d = h.shape
    ff = dn.shape[0]
    whole, left, units = ff // CHUNK, ff % CHUNK, ff // n // 16
    vmem = pl.BlockSpec(memory_space=pltpu.VMEM)
    gu_sum = jax.ShapeDtypeStruct((2, d // n, ff), BF16)
    sems = pltpu.SemaphoreType.DMA((units,))
    return pl.pallas_call(
        functools.partial(first_kernel, n, early),
        out_shape=(gu_sum, gu_sum, jax.ShapeDtypeStruct((2, units, 16, d), BF16)),
        in_specs=[vmem] * 9,
        out_specs=(vmem,) * 3,
        scratch_shapes=work_scratch(tokens, d)
        + sums_scratch(d)
        + [pltpu.VMEM((2, d, ff), BF16), pltpu.VMEM((ff, d), BF16)]
        + [pltpu.VMEM((ff // n, d), BF16)] * 2
        + [sems] * 4
        + ring_scratch(n, whole - early, CHUNK, d)
        + ring_scratch(n, 1, left, d)
        + ring_scratch(n, whole, CHUNK, d)
        + ring_scratch(n, 1, left, d),
        compiler_params=pltpu.CompilerParams(collective_id=2, has_side_effects=True, vmem_limit_bytes=VMEM_LIMIT),
        name="layer0",
    )(h, dh, gu, dn, *old)


def solution(mesh):
    n = mesh.shape["dp"]

    def step(x, dy, *arrays):
        weights, m, v = (arrays[i : i + 3] for i in (0, 3, 6))
        h1, gu0, d0, gu1, d1 = forward(n, x[0], *weights)
        by_h1, *old = backward_last(n, EARLY, h1, dy[0], gu1, d1)
        *sums, by_down = backward_first(n, EARLY, x[0], by_h1, gu0, d0, *old)
        gradients = [g.astype(F32) for g in (*sums, by_down.reshape(weights[2].shape))]
        new = [adamw(w.astype(F32), m, v, g) for w, m, v, g in zip(weights, m, v, gradients, strict=True)]
        return tuple(one[which] for which in range(3) for one in new)

    states, cut = P(("rep", "dp"), None, None), P(None, "dp", None)
    return jax.shard_map(
        step,
        mesh=mesh,
        in_specs=(states, states) + (cut,) * 9,
        out_specs=(P("rep", "dp", None),) * 9,
        check_vma=False,
    )
```

time: 311 us -> 303 us (0.974)
  Pallas kernels: 302 us -> 294 us
  local copies, waits for them, and re-layouts: 3.23 us -> 0.05 us
    pallas_call x1, Pallas kernels: 87 us -> 78.8 us  [forward(): pl.pallas_call(functools.partial(forward_kernel, n), out_shape=(jax.Shape...]
    convert_element_type x3 -> x2, other arithmetic: 4.7 us -> 6.75 us  [adamw(): return ((w - 0.02 * step).astype(BF16), m, v)]
where the time goes in v2:
time: 303 us; the launch traced here: 302 us
  Pallas kernels  294 us (97%)
  other arithmetic  6.75 us (2%)
    pallas_call x1, Pallas kernels, backward_first(): pl.pallas_call(functools.partial(first_kernel, n, early), out_shape=(gu_s...  112 us
    pallas_call x1, Pallas kernels, backward_last(): pl.pallas_call(functools.partial(last_kernel, n, early), out_shape=(jax.S...  104 us
    pallas_call x1, Pallas kernels, forward(): pl.pallas_call(functools.partial(forward_kernel, n), out_shape=(jax.Shape...  78.8 us
    convert_element_type x2, other arithmetic, adamw(): return ((w - 0.02 * step).astype(BF16), m, v)  6.75 us

profile of v2, /device:TPU:22, one launch (start us, length us, event | category | flops | bytes accessed | tf_op | source)
XLA Modules:
  0.0 301.9 jit_solution(16898382953730191277)
XLA Ops:
  0.6 78.8 %gather_forward.1 = (bf16[4096,512]{1,0:T(8,128)(2,1)}, bf16[2,512,1664]{2,1,0:T(8,128)(2,1)}, bf16[1664,512]{1,0:T(8,128)(2,1)}, bf16[2,512,1664]{2,1,0:T(8,128)(2,1)}, bf16[1664,512]{1,0:T(8,128)(2,1)}) custom-call(bf16[4096,512]{1,0:T(8,128)(2,1)} %bitcast.8, bf16[2,64,1664]{2,1,0:T(8,128)(2,1)} %gate_ref.1, bf16[2,64,1664]{2,1,0:T(8,128)(2,1)} %up_ref.1, ...), custom_call_target="tpu_custom_call" | custom-call | tf_op jit(solution)/shard_map/gather_forward/pallas_call | solution.py:196
  79.4 103.7 %layer1.1 = (bf16[4096,512]{1,0:T(8,128)(2,1)}, bf16[2,512,384]{2,1,0:T(8,128)(2,1)}, bf16[384,512]{1,0:T(8,128)(2,1)}, bf16[64,1280]{1,0:T(8,128)(2,1)}, bf16[6...) custom-call(bf16[4096,512]{1,0:T(8,128)(2,1)} %get-tuple-element.23.h_ref, bf16[4096,512]{1,0:T(8,128)(2,1)} %bitcast.10, ...), custom_call_target="tpu_custom_call" | custom-call | tf_op jit(solution)/shard_map/layer1/pallas_call | solution.py:583
  183.2 0.0 copy-start
  183.2 111.8 %layer0.1 = (bf16[2,64,1664]{2,1,0:T(8,128)(2,1)}, bf16[2,64,1664]{2,1,0:T(8,128)(2,1)}, bf16[2,13,16,512]{3,2,1,0:T(8,128)(2,1)}) custom-call(bf16[4096,512]{1,0:T(8,128)(2,1)} %bitcast.9, bf16[4096,512]{1,0:T(8,128)(2,1)} %get-tuple-element.26.dh_ref, bf16[2,512,1664]{2,1,0:T(8,128)(2,1)} %get-tuple-element.27.gu, bf16[1664,512]{1,0:T(8,128)(2,1)} %get-tuple-element.28.dn, ...), custom_call_target="tpu_custom_call" | custom-call | tf_op jit(solution)/shard_map/layer0/pallas_call | solution.py:610
  295.0 0.0 copy-start.1
  295.0 0.0 copy-start.2
  295.0 0.0 copy-start.3
  295.0 0.0 copy-start.4
  295.0 0.0 copy-start.5
  295.0 0.0 copy-start.6
  295.0 0.0 copy-start.7
  295.1 0.0 copy-done
  295.1 3.3 %fusion.10 = (bf16[2,208,512]{2,1,0:T(8,128)(2,1)}, f32[2,208,512]{2,1,0:T(8,128)}, f32[2,208,512]{2,1,0:T(8,128)}) fusion(bf16[2,208,512]{2,1,0:T(8,128)(2,1)S(1)} %copy-done, bf16[2,13,16,512]{3,2,1,0:T(8,128)(2,1)} %get-tuple-element.36, f32[2,208,512]{2,1,0:T(8,128)} %param.21, f32[2,208,512]{2,1,0:T(8,128)} %param.18), kind=kLoop, calls=%fused_computation.23 | loop fusion | flops 3407872 | bytes 4685824 | tf_op jit(solution)/shard_map/convert_element_type | solution.py:35
  298.3 0.0 copy-done.1
  298.3 0.0 copy-done.2
  298.3 0.0 copy-done.3
  298.3 0.0 copy-done.4
  298.4 0.0 copy-done.5
  298.4 0.0 copy-done.6
  298.4 0.0 copy-done.7
  298.4 3.5 %fusion.2 = (bf16[2,64,1664]{2,1,0:T(8,128)(2,1)}, f32[2,64,1664]{2,1,0:T(8,128)}, f32[2,64,1664]{2,1,0:T(8,128)}, bf16[2,64,1664]{2,1,0:T(8,128)(2,1)}, f32[2,64,1664]{2,1,0:T(8,128)}, /*index=5*/f32[2,64,1664]{2,1,0:T(8,128)}) fusion(bf16[2,64,1664]{2,1,0:T(8,128)(2,1)S(1)} %copy-done.1, bf16[2,64,1664]{2,1,0:T(8,128)(2,1)S(1)} %copy-done.7, ...), kind=kLoop, calls=%fused_computation.15 | loop fusion | flops 6815744 | bytes 9371648 | tf_op jit(solution)/shard_map/convert_element_type | solution.py:35
Async XLA Ops:
  183.2 111.9 %copy-start = (bf16[2,208,512]{2,1,0:T(8,128)(2,1)S(1)}, bf16[2,208,512]{2,1,0:T(8,128)(2,1)}, u32[]{:S(2)}) copy-start(bf16[2,208,512]{2,1,0:T(8,128)(2,1)} %down_ref.1) | copy-start | bytes 1277956
  295.0 3.4 %copy-start.1 = (bf16[2,64,1664]{2,1,0:T(8,128)(2,1)S(1)}, bf16[2,64,1664]{2,1,0:T(8,128)(2,1)}, u32[]{:S(2)}) copy-start(bf16[2,64,1664]{2,1,0:T(8,128)(2,1)} %gate_ref.1) | copy-start | bytes 1277956
  295.0 3.4 %copy-start.2 = (bf16[2,64,1664]{2,1,0:T(8,128)(2,1)S(1)}, bf16[2,64,1664]{2,1,0:T(8,128)(2,1)}, u32[]{:S(2)}) copy-start(bf16[2,64,1664]{2,1,0:T(8,128)(2,1)} %up_ref.1) | copy-start | bytes 1277956
  295.0 3.3 %copy-start.3 = (f32[2,64,1664]{2,1,0:T(8,128)S(1)}, f32[2,64,1664]{2,1,0:T(8,128)}, u32[]{:S(2)}) copy-start(f32[2,64,1664]{2,1,0:T(8,128)} %param.19) | copy-start | bytes 2555908
  295.0 3.3 %copy-start.4 = (f32[2,64,1664]{2,1,0:T(8,128)S(1)}, f32[2,64,1664]{2,1,0:T(8,128)}, u32[]{:S(2)}) copy-start(f32[2,64,1664]{2,1,0:T(8,128)} %param.16) | copy-start | bytes 2555908
  295.0 3.3 %copy-start.5 = (f32[2,64,1664]{2,1,0:T(8,128)S(1)}, f32[2,64,1664]{2,1,0:T(8,128)}, u32[]{:S(2)}) copy-start(f32[2,64,1664]{2,1,0:T(8,128)} %param.20) | copy-start | bytes 2555908
  295.0 3.3 %copy-start.6 = (f32[2,64,1664]{2,1,0:T(8,128)S(1)}, f32[2,64,1664]{2,1,0:T(8,128)}, u32[]{:S(2)}) copy-start(f32[2,64,1664]{2,1,0:T(8,128)} %param.17) | copy-start | bytes 2555908
  295.0 3.3 %copy-start.7 = (bf16[2,64,1664]{2,1,0:T(8,128)(2,1)S(1)}, bf16[2,64,1664]{2,1,0:T(8,128)(2,1)}, u32[]{:S(2)}) copy-start(bf16[2,64,1664]{2,1,0:T(8,128)(2,1)} %get-tuple-element.34) | copy-start | bytes 1277956

commit v3 on v2

--- a/solution.py
+++ b/solution.py
@@ -215,84 +215,90 @@
     def __init__(self, n, me, w, gu, dn, base, out_gu, out_dn, bufs):
         self.n, self.me, self.w, self.gu, self.dn, self.base, self.out_gu, self.out_dn = n, me, w, gu, dn, base, out_gu, out_dn
         self.bufs = (bufs[0:3], bufs[3:6])
-        self.rows, self.half = gu.shape[1] // n, dn.shape[1] // 2
+        self.rows = gu.shape[1] // n
         self.far = n // 2
         self.actions = self.far + 1
 
-    def hops(self, p, side):
-        return self.far if side == p else self.n - 1 - self.far
-
-    def part(self, kind, j, p, k):
+    def hops(self, kind, side):
+        return self.far if side == kind else self.n - 1 - self.far
+
+    def part(self, kind, j, k):
         first = self.base + j * self.w
         if kind == 0:
             first = first if isinstance(first, int) else pl.multiple_of(first, self.w)
-            return self.gu.at[p, pl.ds(pl.multiple_of(k * self.rows, self.rows), self.rows), pl.ds(first, self.w)]
+            return self.gu.at[:, pl.ds(pl.multiple_of(k * self.rows, self.rows), self.rows), pl.ds(first, self.w)]
         share = self.w // self.n
-        return self.dn.at[pl.ds(pl.multiple_of(first + k * share, share), share), pl.ds(p * self.half, self.half)]
-
-    def copy(self, kind, j, p, side, src, s):
+        return self.dn.at[pl.ds(pl.multiple_of(first + k * share, share), share)]
+
+    def at(self, kind, side, s):
+        return s if side == 0 else self.hops(kind, 0) + s
+
+    def copy(self, kind, j, side, src, s):
         slots, send, recv = self.bufs[kind]
-        at = s if side == 0 else self.hops(p, 0) + s
+        at = self.at(kind, side, s)
         to = lax.rem(self.me + (1 if side == 0 else self.n - 1), self.n)
-        return pltpu.make_async_remote_copy(src, slots.at[j, p, at], send.at[j, p, at], recv.at[j, p, at], {"dp": to}, MESH)
-
-    def slot(self, kind, j, p, side, s):
-        return self.bufs[kind][0].at[j, p, s if side == 0 else self.hops(p, 0) + s]
+        return pltpu.make_async_remote_copy(src, slots.at[j, at], send.at[j, at], recv.at[j, at], {"dp": to}, MESH)
+
+    def slot(self, kind, j, side, s):
+        return self.bufs[kind][0].at[j, self.at(kind, side, s)]
 
     def step(self, j, s):
         n, me = self.n, self.me
 
-        def whose(p, side, s):
-            left = self.hops(p, side) - s
+        def whose(kind, side, s):
+            left = self.hops(kind, side) - s
             return lax.rem(me + left, n) if side == 0 else lax.rem(me + n - left, n)
 
-        every = [(kind, p, side) for kind in range(2) for p in range(2) for side in range(2)]
+        every = [(kind, side) for kind in range(2) for side in range(2)]
 
         @pl.when(s == 0)
         def _():
-            for kind, p, side in every:
-                self.copy(kind, j, p, side, self.part(kind, j, p, whose(p, side, 0)), 0).start()
+            for kind, side in every:
+                self.copy(kind, j, side, self.part(kind, j, whose(kind, side, 0)), 0).start()
 
         @pl.when((s > 0) & (s < self.far))
         def _():
-            for kind, p, side in every:
-
-                @pl.when(s < self.hops(p, side))
+            for kind, side in every:
+
+                @pl.when(s < self.hops(kind, side))
                 def _():
-                    here = self.slot(kind, j, p, side, s - 1)
-                    self.copy(kind, j, p, side, here, s - 1).wait_recv()
-                    term = self.part(kind, j, p, whose(p, side, s))[...]
+                    here = self.slot(kind, j, side, s - 1)
+                    self.copy(kind, j, side, here, s - 1).wait_recv()
+                    term = self.part(kind, j, whose(kind, side, s))[...]
                     here[...] = (here[...].astype(F32) + term.astype(F32)).astype(BF16)
-                    self.copy(kind, j, p, side, here, s).start()
+                    self.copy(kind, j, side, here, s).start()
 
         @pl.when(s == self.far)
         def _():
             for kind in range(2):
-                for p in range(2):
-                    total = self.part(kind, j, p, me)[...].astype(F32)
-                    for side in range(2):
-                        here = self.slot(kind, j, p, side, self.hops(p, side) - 1)
-                        self.copy(kind, j, p, side, here, self.hops(p, side) - 1).wait_recv()
-                        total += here[...].astype(F32)
-                    (self.out_gu(p, j) if kind == 0 else self.out_dn(p, j))[...] = total.astype(BF16)
+                total = self.part(kind, j, me)[...].astype(F32)
+                for side in range(2):
+                    here = self.slot(kind, j, side, self.hops(kind, side) - 1)
+                    self.copy(kind, j, side, here, self.hops(kind, side) - 1).wait_recv()
+                    total += here[...].astype(F32)
+                total = total.astype(BF16)
+                if kind == 0:
+                    for p in range(2):
+                        self.out_gu(p, j)[...] = total[p]
+                else:
+                    self.out_dn(j)[...] = total
 
     def end(self, count):
         def body(j, _):
             for kind in range(2):
-                for p in range(2):
-                    for side in range(2):
-                        for s in range(self.hops(p, side)):
-                            self.copy(kind, j, p, side, self.slot(kind, j, p, side, s), s).wait_send()
+                for side in range(2):
+                    for s in range(self.hops(kind, side)):
+                        self.copy(kind, j, side, self.slot(kind, j, side, s), s).wait_send()
             return 0
 
         lax.fori_loop(0, count, body, 0)
 
 
 def ring_scratch(n, count, w, d):
-    sems = pltpu.SemaphoreType.DMA((count, 2, n - 1))
+    sems = pltpu.SemaphoreType.DMA((count, n - 1))
     return [
-        pltpu.VMEM((count, 2, n - 1, d // n, w), BF16), sems, sems,
-        pltpu.VMEM((count, 2, n - 1, w // n, d // 2), BF16), sems, sems,
+        pltpu.VMEM((count, n - 1, 2, d // n, w), BF16), sems, sems,
+        pltpu.VMEM((count, n - 1, w // n, d), BF16), sems, sems,
     ]
 
 
@@ -301,8 +307,7 @@
 
 
 def shares(ref, first, n, w):
-    half = ref.shape[1] // 2
-    return lambda side, j: ref.at[pl.ds(pl.multiple_of(first + j * (w // n), w // n), w // n), pl.ds(side * half, half)]
+    return lambda j: ref.at[pl.ds(pl.multiple_of(first + j * (w // n), w // n), w // n)]
 
 
 def rotate3(rings, k, count, tiles):

time: 303 us -> 299 us (0.987)
  no operation moved by 1% of the time
where the time goes in v3:
time: 299 us
  Pallas kernels  291 us (97%)
  other arithmetic  6.75 us (2%)
    pallas_call x1, Pallas kernels, backward_first(): pl.pallas_call(functools.partial(first_kernel, n, early), out_shape=(gu_s...  111 us
    pallas_call x1, Pallas kernels, backward_last(): pl.pallas_call(functools.partial(last_kernel, n, early), out_shape=(jax.S...  101 us
    pallas_call x1, Pallas kernels, forward(): pl.pallas_call(functools.partial(forward_kernel, n), out_shape=(jax.Shape...  78.8 us
    convert_element_type x2, other arithmetic, adamw(): return ((w - 0.02 * step).astype(BF16), m, v)  6.75 us

profile of v3, /device:TPU:22, one launch (start us, length us, event | category | flops | bytes accessed | tf_op | source)
XLA Modules:
  0.0 298.6 jit_solution(383245303391583281)
XLA Ops:
  0.6 78.8 %gather_forward.1 = (bf16[4096,512]{1,0:T(8,128)(2,1)}, bf16[2,512,1664]{2,1,0:T(8,128)(2,1)}, bf16[1664,512]{1,0:T(8,128)(2,1)}, bf16[2,512,1664]{2,1,0:T(8,128)(2,1)}, bf16[1664,512]{1,0:T(8,128)(2,1)}) custom-call(bf16[4096,512]{1,0:T(8,128)(2,1)} %bitcast.8, bf16[2,64,1664]{2,1,0:T(8,128)(2,1)} %gate_ref.1, bf16[2,64,1664]{2,1,0:T(8,128)(2,1)} %up_ref.1, ...), custom_call_target="tpu_custom_call" | custom-call | tf_op jit(solution)/shard_map/gather_forward/pallas_call | solution.py:196
  79.4 101.0 %layer1.1 = (bf16[4096,512]{1,0:T(8,128)(2,1)}, bf16[2,512,384]{2,1,0:T(8,128)(2,1)}, bf16[384,512]{1,0:T(8,128)(2,1)}, bf16[64,1280]{1,0:T(8,128)(2,1)}, bf16[6...) custom-call(bf16[4096,512]{1,0:T(8,128)(2,1)} %get-tuple-element.23.h_ref, bf16[4096,512]{1,0:T(8,128)(2,1)} %bitcast.10, ...), custom_call_target="tpu_custom_call" | custom-call | tf_op jit(solution)/shard_map/layer1/pallas_call | solution.py:588
  180.4 0.0 copy-start
  180.4 111.3 %layer0.1 = (bf16[2,64,1664]{2,1,0:T(8,128)(2,1)}, bf16[2,64,1664]{2,1,0:T(8,128)(2,1)}, bf16[2,13,16,512]{3,2,1,0:T(8,128)(2,1)}) custom-call(bf16[4096,512]{1,0:T(8,128)(2,1)} %bitcast.9, bf16[4096,512]{1,0:T(8,128)(2,1)} %get-tuple-element.26.dh_ref, bf16[2,512,1664]{2,1,0:T(8,128)(2,1)} %get-tuple-element.27.gu, bf16[1664,512]{1,0:T(8,128)(2,1)} %get-tuple-element.28.dn, ...), custom_call_target="tpu_custom_call" | custom-call | tf_op jit(solution)/shard_map/layer0/pallas_call | solution.py:615
  291.7 0.0 copy-start.1
  291.7 0.0 copy-start.2
  291.8 0.0 copy-start.3
  291.8 0.0 copy-start.4
  291.8 0.0 copy-start.5
  291.8 0.0 copy-start.6
  291.8 0.0 copy-start.7
  291.8 0.0 copy-done
  291.8 3.3 %fusion.10 = (bf16[2,208,512]{2,1,0:T(8,128)(2,1)}, f32[2,208,512]{2,1,0:T(8,128)}, f32[2,208,512]{2,1,0:T(8,128)}) fusion(bf16[2,208,512]{2,1,0:T(8,128)(2,1)S(1)} %copy-done, bf16[2,13,16,512]{3,2,1,0:T(8,128)(2,1)} %get-tuple-element.36, f32[2,208,512]{2,1,0:T(8,128)} %param.21, f32[2,208,512]{2,1,0:T(8,128)} %param.18), kind=kLoop, calls=%fused_computation.23 | loop fusion | flops 3407872 | bytes 4685824 | tf_op jit(solution)/shard_map/convert_element_type | solution.py:35
  295.1 0.0 copy-done.1
  295.1 0.0 copy-done.2
  295.1 0.0 copy-done.3
  295.1 0.0 copy-done.4
  295.1 0.0 copy-done.5
  295.1 0.0 copy-done.6
  295.1 0.0 copy-done.7
  295.2 3.5 %fusion.2 = (bf16[2,64,1664]{2,1,0:T(8,128)(2,1)}, f32[2,64,1664]{2,1,0:T(8,128)}, f32[2,64,1664]{2,1,0:T(8,128)}, bf16[2,64,1664]{2,1,0:T(8,128)(2,1)}, f32[2,64,1664]{2,1,0:T(8,128)}, /*index=5*/f32[2,64,1664]{2,1,0:T(8,128)}) fusion(bf16[2,64,1664]{2,1,0:T(8,128)(2,1)S(1)} %copy-done.1, bf16[2,64,1664]{2,1,0:T(8,128)(2,1)S(1)} %copy-done.7, ...), kind=kLoop, calls=%fused_computation.15 | loop fusion | flops 6815744 | bytes 9371648 | tf_op jit(solution)/shard_map/convert_element_type | solution.py:35
Async XLA Ops:
  180.4 111.4 %copy-start = (bf16[2,208,512]{2,1,0:T(8,128)(2,1)S(1)}, bf16[2,208,512]{2,1,0:T(8,128)(2,1)}, u32[]{:S(2)}) copy-start(bf16[2,208,512]{2,1,0:T(8,128)(2,1)} %down_ref.1) | copy-start | bytes 1277956
  291.7 3.4 %copy-start.1 = (bf16[2,64,1664]{2,1,0:T(8,128)(2,1)S(1)}, bf16[2,64,1664]{2,1,0:T(8,128)(2,1)}, u32[]{:S(2)}) copy-start(bf16[2,64,1664]{2,1,0:T(8,128)(2,1)} %gate_ref.1) | copy-start | bytes 1277956
  291.7 3.4 %copy-start.2 = (bf16[2,64,1664]{2,1,0:T(8,128)(2,1)S(1)}, bf16[2,64,1664]{2,1,0:T(8,128)(2,1)}, u32[]{:S(2)}) copy-start(bf16[2,64,1664]{2,1,0:T(8,128)(2,1)} %up_ref.1) | copy-start | bytes 1277956
  291.8 3.3 %copy-start.3 = (f32[2,64,1664]{2,1,0:T(8,128)S(1)}, f32[2,64,1664]{2,1,0:T(8,128)}, u32[]{:S(2)}) copy-start(f32[2,64,1664]{2,1,0:T(8,128)} %param.19) | copy-start | bytes 2555908
  291.8 3.3 %copy-start.4 = (f32[2,64,1664]{2,1,0:T(8,128)S(1)}, f32[2,64,1664]{2,1,0:T(8,128)}, u32[]{:S(2)}) copy-start(f32[2,64,1664]{2,1,0:T(8,128)} %param.16) | copy-start | bytes 2555908
  291.8 3.3 %copy-start.5 = (f32[2,64,1664]{2,1,0:T(8,128)S(1)}, f32[2,64,1664]{2,1,0:T(8,128)}, u32[]{:S(2)}) copy-start(f32[2,64,1664]{2,1,0:T(8,128)} %param.20) | copy-start | bytes 2555908
  291.8 3.3 %copy-start.6 = (f32[2,64,1664]{2,1,0:T(8,128)S(1)}, f32[2,64,1664]{2,1,0:T(8,128)}, u32[]{:S(2)}) copy-start(f32[2,64,1664]{2,1,0:T(8,128)} %param.17) | copy-start | bytes 2555908
  291.8 3.3 %copy-start.7 = (bf16[2,64,1664]{2,1,0:T(8,128)(2,1)S(1)}, bf16[2,64,1664]{2,1,0:T(8,128)(2,1)}, u32[]{:S(2)}) copy-start(bf16[2,64,1664]{2,1,0:T(8,128)(2,1)} %get-tuple-element.34) | copy-start | bytes 1277956
